TPU v7x, 32 devices: a whole 2x2x4 slice. The times are simulated.
32 devices in a mesh: ma: 16 (over z, y, core), freq: 2 (over x).
Axes of the slice: x: 2, y: 2, z: 4, core: 2. Of those that a mesh axis runs over, the one named last changes fastest.
Arguments:
- right_side: float32 [128, 8, 2, 512], P('ma', 'freq'), may hold values from -60 to 60
- start_field: float32 [128, 8, 2, 512], P('ma', 'freq'), may hold values from -6 to 6
- beam: float32 [128, 8, 2, 16, 512], P('ma', 'freq'), may hold values from -0.75 to 0.75
- noise: float32 [128, 8, 16], P('ma', 'freq'), may hold values from 0.3 to 3
- inv_power: float32 [512], replicated, may hold values from 0.5 to 2
- smooth: float32 [512], replicated, may hold values from 0.5 to 4
Outputs:
- solution_field: float32 [128, 8, 2, 512], P('ma', 'freq')
- residual: float32 [128, 8, 2, 512], P('ma', 'freq')
All inputs are finite; a program needn't handle non-finite values.
Results may differ from a plain program's by a relative error of at most 0.0003.
Values sent between devices are 32-bit elements; how exact they have to be, the bound alone decides.
A program may use at most 64 MiB of HBM per device.

v0:
```python
import functools

import jax
import jax.numpy as jnp
from jax import lax
from jax.experimental import pallas as pl
from jax.experimental.pallas import tpu as pltpu
from jax.sharding import PartitionSpec as P

MESH = pl.DeviceIdType.MESH
F32, BF16 = jnp.float32, jnp.bfloat16


def split(x):
    high = x.astype(BF16)
    return high, (x - high.astype(F32)).astype(BF16)


def times(x, high, low, transposed):
    dims = (((1,), (1 if transposed else 0,)), ((), ()))
    rows = x.shape[0]
    x_high, x_low = split(x)
    both = jnp.concatenate([x_high, x_low], axis=0)
    main = lax.dot_general(both, high, dims, preferred_element_type=F32)
    rest = lax.dot_general(x_high, low, dims, preferred_element_type=F32)
    return main[:rows] + (main[rows:] + rest)


def kernel(
    nma, nf, rhs_in, x0_in, beam_in, noise_in, power_in, smooth_in, sol_s, res_s,
    rhs_s, x0_s, beam_s, noise_s, power_s, smooth_s,
    high_s, low_s, x_s, y_s, r_s, u_s, w_s, mask_s, halo_s, message_s, all_s,
    in_sem, beam_sem, halo_send, halo_recv, sum_send, sum_recv, word_sem,
):
    modes, freqs, _, ell = rhs_in.shape
    rank = beam_in.shape[3]
    width = modes * rank
    n = nma * nf
    my_ma, my_f = lax.axis_index("ma"), lax.axis_index("freq")
    me = my_ma * nf + my_f
    last = freqs - 1
    two_sided = nf > 2

    def at(g):
        return jnp.where(my_f == 0, last - g, g)


    x0_copy = pltpu.make_async_copy(x0_in, x0_s, in_sem.at[0])
    small = [
        pltpu.make_async_copy(power_in, power_s, in_sem.at[1]),
        pltpu.make_async_copy(smooth_in, smooth_s, in_sem.at[2]),
        pltpu.make_async_copy(noise_in, noise_s, in_sem.at[3]),
    ]
    rhs_copy = pltpu.make_async_copy(rhs_in, rhs_s, in_sem.at[4])
    x0_copy.start()
    for copy in small:
        copy.start()
    beam_copies = {}
    for f in range(freqs):
        beam_copies[f] = [
            pltpu.make_async_copy(beam_in.at[:, at(f), a], beam_s.at[f, a], beam_sem.at[2 * f + a])
            for a in range(2)
        ]
        for copy in beam_copies[f]:
            copy.start()
        if f == 0:
            rhs_copy.start()

    def target(offset):
        ma = my_ma + offset // nf
        other = my_f + offset % nf
        return lax.rem(ma, nma), lax.rem(other, nf)

    def partners(size, place):
        distances = [1 << bit for bit in range(size.bit_length() - 1)]
        return [place + d * (1 - 2 * (place // d % 2)) for d in distances]

    word = [(my_ma, other) for other in partners(nf, my_f)]
    word += [(other, my_f) for other in partners(nma, my_ma)]
    barrier = pltpu.get_barrier_semaphore()
    near = jnp.where(my_f == 0, 1, my_f - 1)
    has_far = (my_f > 0) & (my_f < nf - 1)

    def greet(device):
        pl.semaphore_signal(barrier, inc=1, device_id=device, device_id_type=MESH)

    for device in word:
        greet(device)
    expected = len(word)
    if nf > 2:
        pl.when(my_f > 0)(lambda: greet((my_ma, my_f - 1)))
        pl.when(my_f < nf - 1)(lambda: greet((my_ma, my_f + 1)))
        expected = expected + jnp.minimum(my_f, 1) + jnp.minimum(nf - 1 - my_f, 1)

    def pass_word(step):
        if step > 0:
            pl.semaphore_wait(word_sem.at[step - 1], 1)
        if step < len(word):
            pl.semaphore_signal(
                word_sem.at[step], inc=1, device_id=word[step], device_id_type=MESH
            )

    def near_copy(kind, source):
        side = jnp.minimum(my_f // 2, 1) if two_sided else 0
        return pltpu.make_async_remote_copy(
            src_ref=source.at[0], dst_ref=halo_s.at[kind, side],
            send_sem=halo_send.at[kind, 0], recv_sem=halo_recv.at[kind, side],
            device_id=(my_ma, near), device_id_type=MESH,
        )

    def far_copy(kind, source):
        return pltpu.make_async_remote_copy(
            src_ref=source.at[last], dst_ref=halo_s.at[kind, 0],
            send_sem=halo_send.at[kind, 1], recv_sem=halo_recv.at[kind, 0],
            device_id=(my_ma, my_f + 1), device_id_type=MESH,
        )

    def arrival(kind, side):
        slot = halo_s.at[kind, side]
        return pltpu.make_async_copy(slot, slot, halo_recv.at[kind, side])

    def send(kind, source):
        if nf > 1:
            near_copy(kind, source).start()
        if two_sided:
            pl.when(has_far)(lambda: far_copy(kind, source).start())

    def arrive(kind):
        if nf > 1:
            arrival(kind, 0).wait()
        if two_sided:
            pl.when(has_far)(lambda: arrival(kind, 1).wait())

    def sent(kind, source):
        if nf > 1:
            near_copy(kind, source).wait_send()
        if two_sided:
            pl.when(has_far)(lambda: far_copy(kind, source).wait_send())

    if nf == 1:
        halo_s[...] = jnp.zeros_like(halo_s)
    if two_sided:
        @pl.when(jnp.logical_not(has_far))
        def _():
            halo_s[:, 1] = jnp.zeros_like(halo_s[:, 1])

    x0_copy.wait()
    for f in range(freqs):
        for b in range(2):
            x_s[f, b * modes:(b + 1) * modes, :] = x0_s[:, at(f), b, :]
    for copy in small:
        copy.wait()
    pl.semaphore_wait(barrier, expected)
    send(0, x_s)
    pass_word(0)

    power, smooth = power_s[...], smooth_s[...]
    own = (
        lax.broadcasted_iota(jnp.int32, (modes, width), 1) // rank
        == lax.broadcasted_iota(jnp.int32, (modes, width), 0)
    )
    for f in range(freqs):
        mask_s[f] = jnp.where(own, jnp.concatenate([noise_s[:, at(f), :]] * modes, axis=1), 0.0)

    def project(f, field):
        seen = times(field, high_s[f], low_s[f], True)
        real = seen[:modes, :width] + seen[modes:, width:]
        imaginary = seen[modes:, :width] - seen[:modes, width:]
        return real, imaginary, mask_s[f] * real, mask_s[f] * imaginary

    def back(f, real, imaginary):
        weighted = jnp.concatenate(
            [
                jnp.concatenate([real, -imaginary], axis=1),
                jnp.concatenate([imaginary, real], axis=1),
            ],
            axis=0,
        )
        return times(weighted, high_s[f], low_s[f], False)

    def count(f):
        value = float(f > 0) + float(f < last) + float(nf > 1 and f == 0)
        if two_sided and f == last:
            value = value + jnp.where(has_far, 1.0, 0.0)
        return value

    def local_prior(f, ref):
        value = count(f) * ref[f]
        if f > 0:
            value = value - ref[f - 1]
        if f < last:
            value = value - ref[f + 1]
        return power * ref[f] + smooth * value

    def apply_beam(f, field):
        _, _, real, imaginary = project(f, field)
        return back(f, real, imaginary)

    steps = list(range(1, len(word) + 1))

    def advance():
        if steps:
            pass_word(steps.pop(0))

    edges = [0, last] if two_sided and last else [0]
    inner = [f for f in range(freqs) if f not in edges]
    for f in edges + inner:
        for copy in beam_copies[f]:
            copy.wait()
        high, low = split(beam_s[f].reshape(2 * width, ell))
        high_s[f] = high
        low_s[f] = low
        if f == 0:
            rhs_copy.wait()
        rhs = jnp.concatenate([rhs_s[:, at(f), 0, :], rhs_s[:, at(f), 1, :]], axis=0)
        y_s[f] = rhs - apply_beam(f, x_s[f]) - local_prior(f, x_s)
        if f == edges[-1]:
            send(1, y_s)
        elif f in inner:
            advance()
    for f in inner:
        r_s[f] = y_s[f]
        u_s[f] = apply_beam(f, r_s[f])
        advance()
    arrive(0)
    arrive(1)
    before = after = 0.0
    r_s[0] = y_s[0] + smooth * halo_s[0, 0]
    if nf > 1:
        before = halo_s[1, 0] + smooth * x_s[0]
    if two_sided:
        base = r_s if last == 0 else y_s
        r_s[last] = base[last] + smooth * halo_s[0, 1]
        after = jnp.where(has_far, halo_s[1, 1] + smooth * x_s[last], 0.0)
    for f in edges:
        value = apply_beam(f, r_s[f]) + local_prior(f, r_s)
        if f == 0:
            value = value - smooth * before
        if f == last:
            value = value - smooth * after
        u_s[f] = value
    send(2, u_s)
    for f in inner:
        u_s[f] = u_s[f] + local_prior(f, r_s)
    norm = jnp.zeros((2 * modes, ell), F32)
    curve, square, cube = norm, norm, norm
    beam_part = jnp.zeros((modes, width), F32)
    pending = {}
    for f in inner + edges:
        real, imaginary, real_weighted, imaginary_weighted = project(f, u_s[f])
        pending[f] = real_weighted, imaginary_weighted
        beam_part = beam_part + (real * real_weighted + imaginary * imaginary_weighted)
        w_s[f] = local_prior(f, u_s)
        norm = norm + r_s[f] * r_s[f]
        curve = curve + r_s[f] * u_s[f]
        square = square + u_s[f] * u_s[f]
        cube = cube + u_s[f] * w_s[f]
    arrive(2)
    before = smooth * halo_s[2, 0]
    cube = cube - before * u_s[0]
    if two_sided:
        after = smooth * halo_s[2, 1]
        cube = cube - after * u_s[last]
    lane = lax.broadcasted_iota(jnp.int32, (1, 128), 1)
    message = jnp.zeros((1, 128), F32)
    for i, part in enumerate((norm, curve, square, cube)):
        total = jnp.sum(part, keepdims=True)
        if i == 3:
            total = total + jnp.sum(beam_part, keepdims=True)
        message = jnp.where(lane == i, total, message)
    message_s[0] = message
    all_s[me] = message

    while steps:
        advance()

    def share(offset, carry):
        pltpu.make_async_remote_copy(
            src_ref=message_s.at[0], dst_ref=all_s.at[me], send_sem=sum_send, recv_sem=sum_recv,
            device_id=target(offset), device_id_type=MESH,
        ).start()
        return carry

    if n > 64:
        lax.fori_loop(1, n, share, 0)
    else:
        for offset in range(1, n):
            share(offset, 0)

    w_s[0] = w_s[0] - before
    if two_sided:
        w_s[last] = w_s[last] - after
    for f in range(freqs):
        w_s[f] = w_s[f] + back(f, *pending[f])
    for kind, source in enumerate((x_s, y_s, u_s)):
        sent(kind, source)
    if n > 1:
        everything = all_s.at[pl.ds(0, n - 1)]
        pltpu.make_async_copy(everything, everything, sum_recv).wait()
    total = jnp.sum(all_s[...], axis=0)
    m0, m1, m2, m3 = (total[:, i:i + 1] for i in range(4))
    step = m0 / m1
    norm_next = step * (step * m2 - m1)
    curve_next = m1 - 2.0 * step * m2 + step * step * m3
    growth = norm_next / m0
    step_next = norm_next / (curve_next - growth * norm_next / step)
    c = step + step_next * (1.0 + growth)
    e = step * step_next
    for f in range(freqs):
        solved = x_s[f] + c * r_s[f] - e * u_s[f]
        left = r_s[f] - c * u_s[f] + e * w_s[f]
        for b in range(2):
            sol_s[:, at(f), b, :] = solved[b * modes:(b + 1) * modes]
            res_s[:, at(f), b, :] = left[b * modes:(b + 1) * modes]
    if n > 1:
        everything = all_s.at[pl.ds(0, n - 1)]
        pltpu.make_async_copy(everything, everything, sum_send).wait()


def write_out(sol_in, res_in, sol_out, res_out, sem):
    copies = [
        pltpu.make_async_copy(sol_in, sol_out, sem.at[0]),
        pltpu.make_async_copy(res_in, res_out, sem.at[1]),
    ]
    for copy in copies:
        copy.start()
    for copy in copies:
        copy.wait()


def shards(right_side, start_field, beam, noise, inv_power, smooth):
    nma, nf = lax.axis_size("ma"), lax.axis_size("freq")
    modes, freqs, _, ell = right_side.shape
    rank = beam.shape[3]
    width = modes * rank
    vmem_spec = pl.BlockSpec(memory_space=pltpu.VMEM)
    any_spec = pl.BlockSpec(memory_space=pl.ANY)
    field = pltpu.VMEM(right_side.shape, F32)
    slab = pltpu.VMEM((freqs, 2 * modes, ell), F32)
    half = pltpu.VMEM((freqs, 2 * width, ell), BF16)
    outs = pl.pallas_call(
        functools.partial(kernel, nma, nf),
        out_shape=[field] * 2,
        in_specs=[any_spec] * 6,
        out_specs=[vmem_spec] * 2,
        scratch_shapes=[
            field, field,
            pltpu.VMEM((freqs, 2, modes, rank, ell), F32),
            pltpu.VMEM(noise.shape, F32),
            pltpu.VMEM((1, ell), F32), pltpu.VMEM((1, ell), F32),
            half, half,
            slab, slab, slab, slab, slab,
            pltpu.VMEM((freqs, modes, width), F32),
            pltpu.VMEM((3, 2, 2 * modes, ell), F32),
            pltpu.VMEM((1, 1, 128), F32),
            pltpu.VMEM((nma * nf, 1, 128), F32),
            pltpu.SemaphoreType.DMA((5,)),
            pltpu.SemaphoreType.DMA((2 * freqs,)),
            pltpu.SemaphoreType.DMA((3, 2)),
            pltpu.SemaphoreType.DMA((3, 2)),
            pltpu.SemaphoreType.DMA,
            pltpu.SemaphoreType.DMA,
            pltpu.SemaphoreType.REGULAR(((nma * nf).bit_length(),)),
        ],
        compiler_params=pltpu.CompilerParams(
            collective_id=0, has_side_effects=True, vmem_limit_bytes=67043328 - 2 * right_side.size * 4
        ),
        name="solve",
    )(right_side, start_field, beam, noise, inv_power[None], smooth[None])
    return pl.pallas_call(
        write_out,
        out_shape=[jax.ShapeDtypeStruct(right_side.shape, F32)] * 2,
        in_specs=[vmem_spec] * 2,
        out_specs=[any_spec] * 2,
        scratch_shapes=[pltpu.SemaphoreType.DMA((2,))],
        compiler_params=pltpu.CompilerParams(vmem_limit_bytes=1024 * 1024),
        name="write_out",
    )(*outs)


def solution(mesh):
    in_specs = (
        P("ma", "freq", None, None),
        P("ma", "freq", None, None),
        P("ma", "freq", None, None, None),
        P("ma", "freq", None),
        P(),
        P(),
    )
    out_specs = (P("ma", "freq", None, None), P("ma", "freq", None, None))
    return jax.shard_map(shards, mesh=mesh, in_specs=in_specs, out_specs=out_specs, check_vma=False)
```

profile of v0, /device:TPU:0, one launch (start us, length us, event | category | flops | bytes accessed | tf_op | source)
XLA Modules:
  0.0 20.8 jit_solution(9539311938214763001)
XLA Ops:
  0.6 19.4 %solve.1 = (f32[8,4,2,512]{3,2,1,0:T(2,128)S(1)}, f32[8,4,2,512]{3,2,1,0:T(2,128)S(1)}) custom-call(f32[8,4,2,512]{3,2,1,0:T(2,128)} %rhs_in.1, f32[8,4,2,512]{3,2,1,0:T(2,128)} %x0_in.1, f32[8,4,2,16,512]{4,3,2,1,0:T(8,128)} %beam_in.1, f32[8,4,16]{2,1,0:T(4,128)} %noise_in.1, f32[1,512]{1,0:T(1,128)} %bitcast.2, f32[1,512]{1,0:T(1,128)} %bitcast.3), custom_call_target="tpu_custom_call" | custom-call | tf_op jit(solution)/shard_map/solve/pallas_call | solution.py:341
  20.1 0.7 %write_out.1 = (f32[8,4,2,512]{3,2,1,0:T(2,128)}, f32[8,4,2,512]{3,2,1,0:T(2,128)}) custom-call(f32[8,4,2,512]{3,2,1,0:T(2,128)S(1)} %get-tuple-element.4.sol_in, f32[8,4,2,512]{3,2,1,0:T(2,128)S(1)} %get-tuple-element.5.res_in), custom_call_target="tpu_custom_call" | custom-call | tf_op jit(solution)/shard_map/write_out/pallas_call | solution.py:370
where the time goes:
time: 20.9 us; the launch traced here: 20.8 us
  Pallas kernels  20.1 us (96%)
  between operations  0.64 us (3%)
    pallas_call x1, Pallas kernels, shards(): pl.pallas_call(functools.partial(kernel, nma, nf), out_shape=[field] * 2,...  19.4 us
    pallas_call x1, Pallas kernels, shards(): pl.pallas_call(write_out, out_shape=[jax.ShapeDtypeStruct(right_side.shap...  0.72 us

commit v1 on v0

v1 whole, which is shorter than its diff:
```python
import functools

import jax
import jax.numpy as jnp
from jax import lax
from jax.experimental import pallas as pl
from jax.experimental.pallas import tpu as pltpu
from jax.sharding import PartitionSpec as P

MESH = pl.DeviceIdType.MESH
F32, BF16 = jnp.float32, jnp.bfloat16


def split(x):
    high = x.astype(BF16)
    return high, (x - high.astype(F32)).astype(BF16)


def times(x, high, low, transposed):
    dims = (((1,), (1 if transposed else 0,)), ((), ()))
    rows = x.shape[0]
    x_high, x_low = split(x)
    both = jnp.concatenate([x_high, x_low], axis=0)
    main = lax.dot_general(both, high, dims, preferred_element_type=F32)
    rest = lax.dot_general(x_high, low, dims, preferred_element_type=F32)
    return main[:rows] + (main[rows:] + rest)


def total_of(x):
    return jnp.sum(jnp.sum(x, axis=0, keepdims=True), axis=1, keepdims=True)


def kernel(
    nma, nf, rhs_in, x0_in, beam_in, noise_in, power_in, smooth_in, sol_s, res_s,
    rhs_s, x0_s, edge_s, beam_s, noise_s, power_s, smooth_s,
    high_s, low_s, x_s, y_s, r_s, v_s, u_s, w_s, mask_s, first_s, halo_s,
    sol_move_s, res_move_s, message_s, early_s, late_s,
    in_sem, beam_sem, halo_send, halo_recv, sum_send, sum_recv, word_sem,
):
    modes, freqs, _, ell = rhs_in.shape
    rank = beam_in.shape[3]
    width = modes * rank
    n = nma * nf
    my_ma, my_f = lax.axis_index("ma"), lax.axis_index("freq")
    me = my_ma * nf + my_f
    last = freqs - 1
    two_sided = nf > 2
    edges = [0, last][:min(nf - 1, 2)]
    inner = [f for f in range(freqs) if f not in edges]

    def at(g):
        return jnp.where(my_f == 0, last - g, g)

    edge_copies = [
        pltpu.make_async_copy(x0_in.at[:, at(f)], edge_s.at[i], in_sem.at[i])
        for i, f in enumerate(edges)
    ]
    x0_copy = pltpu.make_async_copy(x0_in, x0_s, in_sem.at[2])
    rhs_copy = pltpu.make_async_copy(rhs_in, rhs_s, in_sem.at[3])
    small = [
        pltpu.make_async_copy(power_in, power_s, in_sem.at[4]),
        pltpu.make_async_copy(smooth_in, smooth_s, in_sem.at[5]),
        pltpu.make_async_copy(noise_in, noise_s, in_sem.at[6]),
    ]
    beam_copies = [
        pltpu.make_async_copy(beam_in.at[:, at(f)], beam_s.at[f], beam_sem.at[f])
        for f in range(freqs)
    ]
    for copy in edge_copies + [x0_copy] + small + [beam_copies[0], rhs_copy] + beam_copies[1:]:
        copy.start()

    def partners(size, place):
        distances = [1 << bit for bit in range(size.bit_length() - 1)]
        return [place + d * (1 - 2 * (place // d % 2)) for d in distances]

    word = [(my_ma, other) for other in partners(nf, my_f)]
    word += [(other, my_f) for other in partners(nma, my_ma)]
    words = max(len(word) - 1, 0)
    barrier = pltpu.get_barrier_semaphore()
    near = jnp.where(my_f == 0, 1, my_f - 1)
    has_far = (my_f > 0) & (my_f < nf - 1)

    def greet(device):
        pl.semaphore_signal(barrier, inc=1, device_id=device, device_id_type=MESH)

    for device in word:
        greet(device)
    expected = len(word)
    if nf > 2:
        pl.when(my_f > 0)(lambda: greet((my_ma, my_f - 1)))
        pl.when(my_f < nf - 1)(lambda: greet((my_ma, my_f + 1)))
        expected = expected + jnp.minimum(my_f, 1) + jnp.minimum(nf - 1 - my_f, 1)

    steps = list(range(words + 1))

    def advance():
        if steps:
            step = steps.pop(0)
            if step > 0:
                pl.semaphore_wait(word_sem.at[step - 1], 1)
            if step < words:
                pl.semaphore_signal(
                    word_sem.at[step], inc=1, device_id=word[step], device_id_type=MESH
                )

    slots = [(edge_s, first_s), (y_s, halo_s.at[0]), (v_s, halo_s.at[1])]

    def near_copy(kind):
        source, target = slots[kind]
        side = jnp.minimum(my_f // 2, 1) if two_sided else 0
        return pltpu.make_async_remote_copy(
            src_ref=source.at[0], dst_ref=target.at[side],
            send_sem=halo_send.at[kind, 0], recv_sem=halo_recv.at[kind, side],
            device_id=(my_ma, near), device_id_type=MESH,
        )

    def far_copy(kind):
        source, target = slots[kind]
        return pltpu.make_async_remote_copy(
            src_ref=source.at[1], dst_ref=target.at[0],
            send_sem=halo_send.at[kind, 1], recv_sem=halo_recv.at[kind, 0],
            device_id=(my_ma, my_f + 1), device_id_type=MESH,
        )

    def arrival(kind, side):
        slot = slots[kind][1].at[side]
        return pltpu.make_async_copy(slot, slot, halo_recv.at[kind, side])

    def send(kind):
        if nf > 1:
            near_copy(kind).start()
        if two_sided:
            pl.when(has_far)(lambda: far_copy(kind).start())

    def arrive(kind):
        if nf > 1:
            arrival(kind, 0).wait()
        if two_sided:
            pl.when(has_far)(lambda: arrival(kind, 1).wait())

    def sent(kind):
        if nf > 1:
            near_copy(kind).wait_send()
        if two_sided:
            pl.when(has_far)(lambda: far_copy(kind).wait_send())

    def beside(i, value):
        return jnp.where(has_far, value, 0.0) if i else value

    if two_sided:
        @pl.when(jnp.logical_not(has_far))
        def _():
            first_s[1] = jnp.zeros_like(first_s[1])
            halo_s[:, 1] = jnp.zeros_like(halo_s[:, 1])

    for copy in edge_copies:
        copy.wait()
    pl.semaphore_wait(barrier, expected)
    send(0)
    advance()

    x0_copy.wait()
    for copy in small:
        copy.wait()
    for f in range(freqs):
        for b in range(2):
            x_s[f, b * modes:(b + 1) * modes, :] = x0_s[:, at(f), b, :]
    power, smooth = power_s[...], smooth_s[...]
    own = (
        lax.broadcasted_iota(jnp.int32, (modes, width), 1) // rank
        == lax.broadcasted_iota(jnp.int32, (modes, width), 0)
    )
    for f in range(freqs):
        mask_s[f] = jnp.where(own, jnp.concatenate([noise_s[:, at(f), :]] * modes, axis=1), 0.0)

    def project(f, field):
        seen = times(field, high_s[f], low_s[f], True)
        real = seen[:modes, :width] + seen[modes:, width:]
        imaginary = seen[modes:, :width] - seen[:modes, width:]
        return real, imaginary, mask_s[f] * real, mask_s[f] * imaginary

    def back(f, real, imaginary):
        weighted = jnp.concatenate(
            [
                jnp.concatenate([real, -imaginary], axis=1),
                jnp.concatenate([imaginary, real], axis=1),
            ],
            axis=0,
        )
        return times(weighted, high_s[f], low_s[f], False)

    def apply_beam(fs, fields):
        parts = [project(f, field) for f, field in zip(fs, fields)]
        return [back(f, *part[2:]) for f, part in zip(fs, parts)]

    def count(f):
        value = float(f > 0) + float(f < last) + float(nf > 1 and f == 0)
        if two_sided and f == last:
            value = value + jnp.where(has_far, 1.0, 0.0)
        return value

    def local_prior(f, ref):
        value = count(f) * ref[f]
        if f > 0:
            value = value - ref[f - 1]
        if f < last:
            value = value - ref[f + 1]
        return power * ref[f] + smooth * value

    for copy in beam_copies:
        copy.wait()
    rhs_copy.wait()
    for f in range(freqs):
        for a in range(2):
            rows = slice(a * width, (a + 1) * width)
            high, low = split(beam_s[f, :, a].reshape(width, ell))
            high_s[f, rows] = high
            low_s[f, rows] = low
    order = edges + inner
    images = apply_beam(order, [x_s[f] for f in order])
    for f, image in zip(order, images):
        rhs = jnp.concatenate([rhs_s[:, at(f), 0, :], rhs_s[:, at(f), 1, :]], axis=0)
        value = rhs - image - local_prior(f, x_s)
        if f in edges:
            y_s[edges.index(f)] = value
        else:
            r_s[f] = value
    send(1)
    advance()

    for f, image in zip(inner, apply_beam(inner, [r_s[f] for f in inner])):
        u_s[f] = image
    advance()

    arrive(0)
    for i, f in enumerate(edges):
        halo = jnp.concatenate([first_s[i, :, 0, :], first_s[i, :, 1, :]], axis=0)
        r_s[f] = y_s[i] + smooth * halo
    for i, (f, image) in enumerate(zip(edges, apply_beam(edges, [r_s[f] for f in edges]))):
        v_s[i] = image + local_prior(f, r_s)
    send(2)
    advance()

    for f in inner:
        u_s[f] = u_s[f] + local_prior(f, r_s)
    seen = {f: project(f, u_s[f]) for f in inner}
    advance()

    arrive(1)
    for i, f in enumerate(edges):
        u_s[f] = v_s[i] - beside(i, smooth * (halo_s[0, i] + smooth * x_s[f]))
    for f in edges:
        seen[f] = project(f, u_s[f])
    norm = jnp.zeros((2 * modes, ell), F32)
    curve, square, cube = norm, norm, norm
    beam_part = jnp.zeros((modes, width), F32)
    for f in inner + edges:
        real, imaginary, real_weighted, imaginary_weighted = seen[f]
        beam_part = beam_part + (real * real_weighted + imaginary * imaginary_weighted)
        w_s[f] = local_prior(f, u_s)
        norm = norm + r_s[f] * r_s[f]
        curve = curve + r_s[f] * u_s[f]
        square = square + u_s[f] * u_s[f]
        cube = cube + u_s[f] * w_s[f]
    lane = lax.broadcasted_iota(jnp.int32, (1, 128), 1)
    message = jnp.zeros((1, 128), F32)
    for i, part in enumerate((norm, curve, square, cube)):
        total = total_of(part)
        if i == 3:
            total = total + total_of(beam_part)
        message = jnp.where(lane == i, total, message)
    message_s[0] = message
    early_s[me] = message

    while steps:
        advance()

    def share(source, target, turn, offset):
        slot = my_ma if turn and nf == 2 else me
        pltpu.make_async_remote_copy(
            src_ref=message_s.at[source], dst_ref=target.at[slot],
            send_sem=sum_send.at[turn], recv_sem=sum_recv.at[turn],
            device_id=(lax.rem(my_ma + offset // nf, nma), lax.rem(my_f + offset % nf, nf)),
            device_id_type=MESH,
        ).start()

    def share_all(source, target, turn):
        stride = nf if turn and nf == 2 else 1
        if n > 64:
            def body(i, carry):
                share(source, target, turn, i * stride)
                return carry

            lax.fori_loop(1, n // stride, body, 0)
        else:
            offsets = range(stride, n, stride)
            for offset in sorted(offsets, key=lambda o: abs(2 * (o // nf) - nma)):
                share(source, target, turn, offset)

    def landed(target, sem):
        count_in = target.shape[0] - 1
        if count_in:
            rows = target.at[pl.ds(0, count_in)]
            pltpu.make_async_copy(rows, rows, sem).wait()

    share_all(0, early_s, 0)
    for f in inner + edges:
        w_s[f] = w_s[f] + back(f, *seen[f][2:])

    arrive(2)
    cross = jnp.zeros((2 * modes, ell), F32)
    nexts = []
    for i, f in enumerate(edges):
        pull = beside(i, smooth * (halo_s[1, i] - smooth * r_s[f]))
        nexts.append(pull)
        cross = cross + pull * u_s[f]
    message = jnp.sum(cross, axis=0, keepdims=True)
    message = sum(message[:, i:i + 128] for i in range(0, ell, 128))
    late_s[my_ma if nf == 2 else me] = message
    message_s[1] = message
    share_all(1, late_s, 1)
    for f, pull in zip(edges, nexts):
        w_s[f] = w_s[f] - pull

    for kind in range(3):
        sent(kind)
    landed(early_s, sum_recv.at[0])
    total = jnp.sum(early_s[...], axis=0)
    m0, m1, m2, m3 = (
        jnp.sum(jnp.where(lane == i, total, 0.0), axis=1, keepdims=True) for i in range(4)
    )
    step = m0 / m1
    norm_next = step * (step * m2 - m1)
    growth = norm_next / m0
    curve_part = m1 - 2.0 * step * m2 + step * step * m3 - growth * norm_next / step
    cross_scale = step * step * (2.0 if nf == 2 else 1.0)
    for f in range(freqs):
        x, r, u, w = x_s[f], r_s[f], u_s[f], w_s[f]
        for b in range(2):
            rows = slice(b * modes, (b + 1) * modes)
            sol_s[:, at(f), b, :] = x[rows] + step * r[rows]
            res_s[:, at(f), b, :] = r[rows] - step * u[rows]
            sol_move_s[:, at(f), b, :] = (1.0 + growth) * r[rows] - step * u[rows]
            res_move_s[:, at(f), b, :] = (1.0 + growth) * u[rows] - step * w[rows]
    landed(early_s, sum_send.at[0])
    landed(late_s, sum_send.at[1])

    landed(late_s, sum_recv.at[1])
    crossed = jnp.sum(jnp.sum(late_s[...], axis=0), axis=1, keepdims=True)
    step_next = norm_next / (curve_part - cross_scale * crossed)
    sol_s[...] = sol_s[...] + step_next * sol_move_s[...]
    res_s[...] = res_s[...] - step_next * res_move_s[...]


def write_out(sol_in, res_in, sol_out, res_out, sem):
    copies = [
        pltpu.make_async_copy(sol_in, sol_out, sem.at[0]),
        pltpu.make_async_copy(res_in, res_out, sem.at[1]),
    ]
    for copy in copies:
        copy.start()
    for copy in copies:
        copy.wait()


def shards(right_side, start_field, beam, noise, inv_power, smooth):
    nma, nf = lax.axis_size("ma"), lax.axis_size("freq")
    modes, freqs, _, ell = right_side.shape
    rank = beam.shape[3]
    width = modes * rank
    sides = 2 if nf > 2 else 1
    vmem_spec = pl.BlockSpec(memory_space=pltpu.VMEM)
    any_spec = pl.BlockSpec(memory_space=pl.ANY)
    field = pltpu.VMEM(right_side.shape, F32)
    edge = pltpu.VMEM((sides, modes, 2, ell), F32)
    slab = pltpu.VMEM((freqs, 2 * modes, ell), F32)
    edge_slab = pltpu.VMEM((sides, 2 * modes, ell), F32)
    half = pltpu.VMEM((freqs, 2 * width, ell), BF16)
    outs = pl.pallas_call(
        functools.partial(kernel, nma, nf),
        out_shape=[field] * 2,
        in_specs=[any_spec] * 6,
        out_specs=[vmem_spec] * 2,
        scratch_shapes=[
            field, field, edge,
            pltpu.VMEM((freqs, modes, 2, rank, ell), F32),
            pltpu.VMEM(noise.shape, F32),
            pltpu.VMEM((1, ell), F32), pltpu.VMEM((1, ell), F32),
            half, half,
            slab, edge_slab, slab, edge_slab, slab, slab,
            pltpu.VMEM((freqs, modes, width), F32),
            edge,
            pltpu.VMEM((2, sides, 2 * modes, ell), F32),
            field, field,
            pltpu.VMEM((2, 1, 128), F32),
            pltpu.VMEM((nma * nf, 1, 128), F32),
            pltpu.VMEM((nma if nf == 2 else nma * nf, 1, 128), F32),
            pltpu.SemaphoreType.DMA((7,)),
            pltpu.SemaphoreType.DMA((freqs,)),
            pltpu.SemaphoreType.DMA((3, sides)),
            pltpu.SemaphoreType.DMA((3, sides)),
            pltpu.SemaphoreType.DMA((2,)),
            pltpu.SemaphoreType.DMA((2,)),
            pltpu.SemaphoreType.REGULAR((max((nma * nf).bit_length() - 2, 1),)),
        ],
        compiler_params=pltpu.CompilerParams(
            collective_id=0, has_side_effects=True, vmem_limit_bytes=67043328 - 2 * right_side.size * 4
        ),
        name="solve",
    )(right_side, start_field, beam, noise, inv_power[None], smooth[None])
    return pl.pallas_call(
        write_out,
        out_shape=[jax.ShapeDtypeStruct(right_side.shape, F32)] * 2,
        in_specs=[vmem_spec] * 2,
        out_specs=[any_spec] * 2,
        scratch_shapes=[pltpu.SemaphoreType.DMA((2,))],
        compiler_params=pltpu.CompilerParams(vmem_limit_bytes=1024 * 1024),
        name="write_out",
    )(*outs)


def solution(mesh):
    in_specs = (
        P("ma", "freq", None, None),
        P("ma", "freq", None, None),
        P("ma", "freq", None, None, None),
        P("ma", "freq", None),
        P(),
        P(),
    )
    out_specs = (P("ma", "freq", None, None), P("ma", "freq", None, None))
    return jax.shard_map(shards, mesh=mesh, in_specs=in_specs, out_specs=out_specs, check_vma=False)
```

time: 20.9 us -> 17.6 us (0.84)
  Pallas kernels: 20.1 us -> 16.8 us
    pallas_call x1, Pallas kernels: 19.4 us -> 16.1 us  [shards(): pl.pallas_call(functools.partial(kernel, nma, nf), out_shape=[field] * 2,...]
where the time goes in v1:
time: 17.6 us; the launch traced here: 17.5 us
  Pallas kernels  16.8 us (95%)
  between operations  0.64 us (4%)
    pallas_call x1, Pallas kernels, shards(): pl.pallas_call(functools.partial(kernel, nma, nf), out_shape=[field] * 2,...  16.1 us
    pallas_call x1, Pallas kernels, shards(): pl.pallas_call(write_out, out_shape=[jax.ShapeDtypeStruct(right_side.shap...  0.72 us

profile of v1, /device:TPU:0, one launch (start us, length us, event | category | flops | bytes accessed | tf_op | source)
XLA Modules:
  0.0 17.5 jit_solution(16597179447802564102)
XLA Ops:
  0.6 16.1 %solve.1 = (f32[8,4,2,512]{3,2,1,0:T(2,128)S(1)}, f32[8,4,2,512]{3,2,1,0:T(2,128)S(1)}) custom-call(f32[8,4,2,512]{3,2,1,0:T(2,128)} %rhs_in.1, f32[8,4,2,512]{3,2,1,0:T(2,128)} %x0_in.1, f32[8,4,2,16,512]{4,3,2,1,0:T(8,128)} %beam_in.1, f32[8,4,16]{2,1,0:T(4,128)} %noise_in.1, f32[1,512]{1,0:T(1,128)} %bitcast.2, f32[1,512]{1,0:T(1,128)} %bitcast.3), custom_call_target="tpu_custom_call" | custom-call | tf_op jit(solution)/shard_map/solve/pallas_call | solution.py:379
  16.8 0.7 %write_out.1 = (f32[8,4,2,512]{3,2,1,0:T(2,128)}, f32[8,4,2,512]{3,2,1,0:T(2,128)}) custom-call(f32[8,4,2,512]{3,2,1,0:T(2,128)S(1)} %get-tuple-element.4.sol_in, f32[8,4,2,512]{3,2,1,0:T(2,128)S(1)} %get-tuple-element.5.res_in), custom_call_target="tpu_custom_call" | custom-call | tf_op jit(solution)/shard_map/write_out/pallas_call | solution.py:411

commit v2 on v1

--- a/solution.py
+++ b/solution.py
@@ -26,6 +26,26 @@
     return main[:rows] + (main[rows:] + rest)
 
 
+def folded(parts):
+    row = lax.broadcasted_iota(jnp.int32, parts[0].shape, 0)
+    upper = row < 4
+    fours = [
+        jnp.where(upper, parts[s], parts[s + 4])
+        + pltpu.roll(jnp.where(upper, parts[s + 4], parts[s]), 4, 0)
+        for s in range(4)
+    ]
+    even = row // 2 % 2 == 0
+    twos = [
+        jnp.where(
+            even, fours[s] + pltpu.roll(fours[s], 6, 0), fours[s + 2] + pltpu.roll(fours[s + 2], 2, 0)
+        )
+        for s in range(2)
+    ]
+    return jnp.where(
+        row % 2 == 0, twos[0] + pltpu.roll(twos[0], 7, 0), twos[1] + pltpu.roll(twos[1], 1, 0)
+    )
+
+
 def total_of(x):
     return jnp.sum(jnp.sum(x, axis=0, keepdims=True), axis=1, keepdims=True)
 
@@ -33,7 +53,7 @@
 def kernel(
     nma, nf, rhs_in, x0_in, beam_in, noise_in, power_in, smooth_in, sol_s, res_s,
     rhs_s, x0_s, edge_s, beam_s, noise_s, power_s, smooth_s,
-    high_s, low_s, x_s, y_s, r_s, v_s, u_s, w_s, mask_s, first_s, halo_s,
+    high_s, low_s, x_s, y_s, r_s, v_s, u_s, w_s, mask_s, column_s, first_s, halo_s,
     sol_move_s, res_move_s, message_s, early_s, late_s,
     in_sem, beam_sem, halo_send, halo_recv, sum_send, sum_recv, word_sem,
 ):
@@ -45,6 +65,7 @@
     me = my_ma * nf + my_f
     last = freqs - 1
     two_sided = nf > 2
+    groups = modes // 4
     edges = [0, last][:min(nf - 1, 2)]
     inner = [f for f in range(freqs) if f not in edges]
 
@@ -103,46 +124,52 @@
                     word_sem.at[step], inc=1, device_id=word[step], device_id_type=MESH
                 )
 
-    slots = [(edge_s, first_s), (y_s, halo_s.at[0]), (v_s, halo_s.at[1])]
-
-    def near_copy(kind):
-        source, target = slots[kind]
+    def piece(kind, g):
+        if kind == 0:
+            rows = pl.ds(4 * g, 4)
+            return (lambda i: edge_s.at[i, rows]), (lambda i: first_s.at[i, rows])
+        source = (y_s, v_s)[kind - 1]
+        rows = pl.ds(8 * g, 8)
+        return (lambda i: source.at[i, rows]), (lambda i: halo_s.at[kind - 1, i, rows])
+
+    def near_copy(kind, g):
+        source, target = piece(kind, g)
         side = jnp.minimum(my_f // 2, 1) if two_sided else 0
         return pltpu.make_async_remote_copy(
-            src_ref=source.at[0], dst_ref=target.at[side],
-            send_sem=halo_send.at[kind, 0], recv_sem=halo_recv.at[kind, side],
+            src_ref=source(0), dst_ref=target(side),
+            send_sem=halo_send.at[kind, g, 0], recv_sem=halo_recv.at[kind, g, side],
             device_id=(my_ma, near), device_id_type=MESH,
         )
 
-    def far_copy(kind):
-        source, target = slots[kind]
+    def far_copy(kind, g):
+        source, target = piece(kind, g)
         return pltpu.make_async_remote_copy(
-            src_ref=source.at[1], dst_ref=target.at[0],
-            send_sem=halo_send.at[kind, 1], recv_sem=halo_recv.at[kind, 0],
+            src_ref=source(1), dst_ref=target(0),
+            send_sem=halo_send.at[kind, g, 1], recv_sem=halo_recv.at[kind, g, 0],
             device_id=(my_ma, my_f + 1), device_id_type=MESH,
         )
 
-    def arrival(kind, side):
-        slot = slots[kind][1].at[side]
-        return pltpu.make_async_copy(slot, slot, halo_recv.at[kind, side])
-
-    def send(kind):
+    def arrival(kind, g, side):
+        slot = piece(kind, g)[1](side)
+        return pltpu.make_async_copy(slot, slot, halo_recv.at[kind, g, side])
+
+    def send(kind, g):
         if nf > 1:
-            near_copy(kind).start()
+            near_copy(kind, g).start()
         if two_sided:
-            pl.when(has_far)(lambda: far_copy(kind).start())
-
-    def arrive(kind):
+            pl.when(has_far)(lambda: far_copy(kind, g).start())
+
+    def arrive(kind, g):
         if nf > 1:
-            arrival(kind, 0).wait()
+            arrival(kind, g, 0).wait()
         if two_sided:
-            pl.when(has_far)(lambda: arrival(kind, 1).wait())
-
-    def sent(kind):
+            pl.when(has_far)(lambda: arrival(kind, g, 1).wait())
+
+    def sent(kind, g):
         if nf > 1:
-            near_copy(kind).wait_send()
+            near_copy(kind, g).wait_send()
         if two_sided:
-            pl.when(has_far)(lambda: far_copy(kind).wait_send())
+            pl.when(has_far)(lambda: far_copy(kind, g).wait_send())
 
     def beside(i, value):
         return jnp.where(has_far, value, 0.0) if i else value
@@ -156,42 +183,97 @@
     for copy in edge_copies:
         copy.wait()
     pl.semaphore_wait(barrier, expected)
-    send(0)
+    for g in range(groups):
+        send(0, g)
     advance()
 
     x0_copy.wait()
     for copy in small:
         copy.wait()
-    for f in range(freqs):
-        for b in range(2):
-            x_s[f, b * modes:(b + 1) * modes, :] = x0_s[:, at(f), b, :]
-    power, smooth = power_s[...], smooth_s[...]
-    own = (
-        lax.broadcasted_iota(jnp.int32, (modes, width), 1) // rank
-        == lax.broadcasted_iota(jnp.int32, (modes, width), 0)
-    )
-    for f in range(freqs):
-        mask_s[f] = jnp.where(own, jnp.concatenate([noise_s[:, at(f), :]] * modes, axis=1), 0.0)
-
-    def project(f, field):
-        seen = times(field, high_s[f], low_s[f], True)
-        real = seen[:modes, :width] + seen[modes:, width:]
-        imaginary = seen[modes:, :width] - seen[:modes, width:]
-        return real, imaginary, mask_s[f] * real, mask_s[f] * imaginary
-
-    def back(f, real, imaginary):
-        weighted = jnp.concatenate(
-            [
-                jnp.concatenate([real, -imaginary], axis=1),
-                jnp.concatenate([imaginary, real], axis=1),
-            ],
+    def rows_of(ref, *at_f):
+        place = (slice(None), *at_f)
+        return jnp.concatenate(
+            [ref[(slice(4 * g, 4 * g + 4), *place[1:], b)] for g in range(groups) for b in range(2)],
             axis=0,
         )
-        return times(weighted, high_s[f], low_s[f], False)
+
+    def group(g):
+        return slice(8 * g, 8 * g + 8)
+
+    for f in range(freqs):
+        x_s[f] = rows_of(x0_s, at(f))
+    power, smooth = power_s[...], smooth_s[...]
+    row = lax.broadcasted_iota(jnp.int32, (2 * modes, width), 0)
+    own = lax.broadcasted_iota(jnp.int32, (2 * modes, width), 1) // rank == row // 8 * 4 + row % 4
+    sign = jnp.where(row % 8 < 4, 1.0, -1.0)
+    for i, f in enumerate(inner):
+        levels = noise_s[:, at(f), :]
+        levels = jnp.concatenate(
+            [levels[4 * g:4 * g + 4] for g in range(groups) for _ in range(2)], axis=0
+        )
+        mask_s[i] = jnp.where(own, jnp.concatenate([levels] * modes, axis=1), 0.0)
+    unit = (
+        lax.broadcasted_iota(jnp.int32, (rank, rank), 0)
+        == lax.broadcasted_iota(jnp.int32, (rank, rank), 1)
+    )
+    for i, f in enumerate(edges):
+        levels = noise_s[:, at(f), :]
+        for m in range(modes):
+            column = jnp.sum(jnp.where(unit, levels[m:m + 1], 0.0), axis=1, keepdims=True)
+            column_s[i, m] = jnp.broadcast_to(column, (rank, 128))
+
+    def swapped(x):
+        return jnp.concatenate([pltpu.roll(x[group(g)], 4, 0) for g in range(groups)], axis=0)
+
+    def project(f, field):
+        i = inner.index(f)
+        seen = times(field, high_s[i], low_s[i], True)
+        parts = seen[:, :width] + sign * swapped(seen[:, width:])
+        return parts, mask_s[i] * parts
+
+    def back(f, weighted):
+        i = inner.index(f)
+        weighted = jnp.concatenate([weighted, -sign * swapped(weighted)], axis=1)
+        return times(weighted, high_s[i], low_s[i], False)
 
     def apply_beam(fs, fields):
         parts = [project(f, field) for f, field in zip(fs, fields)]
-        return [back(f, *part[2:]) for f, part in zip(fs, parts)]
+        return [back(f, part[1]) for f, part in zip(fs, parts)]
+
+    def wide(x):
+        return jnp.concatenate([x] * (ell // 128), axis=1)
+
+    def edge_project(f, g, field):
+        parts = []
+        for j in range(4):
+            m = 4 * g + j
+            real_beam, imaginary_beam = beam_s[f, m, 0], beam_s[f, m, 1]
+            real_field, imaginary_field = field[j:j + 1], field[4 + j:5 + j]
+            levels = column_s[edges.index(f), m]
+            real = jnp.sum(
+                real_beam * real_field + imaginary_beam * imaginary_field, axis=1, keepdims=True
+            )
+            imaginary = jnp.sum(
+                real_beam * imaginary_field - imaginary_beam * real_field, axis=1, keepdims=True
+            )
+            parts.append((real, imaginary, levels * real, levels * imaginary))
+        return parts
+
+    def edge_back(f, g, parts):
+        reals, imaginaries = [], []
+        for j, (_, _, real, imaginary) in enumerate(parts):
+            m = 4 * g + j
+            real, imaginary = wide(real), wide(imaginary)
+            real_beam, imaginary_beam = beam_s[f, m, 0], beam_s[f, m, 1]
+            for found, value in (
+                (reals, real_beam * real - imaginary_beam * imaginary),
+                (imaginaries, real_beam * imaginary + imaginary_beam * real),
+            ):
+                found.append(sum(value[k:k + 8] for k in range(0, rank, 8)))
+        return folded(reals + imaginaries)
+
+    def edge_beam(f, g, field):
+        return edge_back(f, g, edge_project(f, g, field))
 
     def count(f):
         value = float(f > 0) + float(f < last) + float(nf > 1 and f == 0)
@@ -199,46 +281,48 @@
             value = value + jnp.where(has_far, 1.0, 0.0)
         return value
 
-    def local_prior(f, ref):
-        value = count(f) * ref[f]
+    def local_prior(f, ref, rows=slice(None)):
+        value = count(f) * ref[f, rows]
         if f > 0:
-            value = value - ref[f - 1]
+            value = value - ref[f - 1, rows]
         if f < last:
-            value = value - ref[f + 1]
-        return power * ref[f] + smooth * value
+            value = value - ref[f + 1, rows]
+        return power * ref[f, rows] + smooth * value
 
     for copy in beam_copies:
         copy.wait()
     rhs_copy.wait()
-    for f in range(freqs):
+    for i, f in enumerate(inner):
         for a in range(2):
             rows = slice(a * width, (a + 1) * width)
             high, low = split(beam_s[f, :, a].reshape(width, ell))
-            high_s[f, rows] = high
-            low_s[f, rows] = low
-    order = edges + inner
-    images = apply_beam(order, [x_s[f] for f in order])
-    for f, image in zip(order, images):
-        rhs = jnp.concatenate([rhs_s[:, at(f), 0, :], rhs_s[:, at(f), 1, :]], axis=0)
-        value = rhs - image - local_prior(f, x_s)
-        if f in edges:
-            y_s[edges.index(f)] = value
-        else:
-            r_s[f] = value
-    send(1)
+            high_s[i, rows] = high
+            low_s[i, rows] = low
+    images = apply_beam(inner, [x_s[f] for f in inner])
+    for i, f in enumerate(edges):
+        for g in range(groups):
+            rows = group(g)
+            image = edge_beam(f, g, x_s[f, rows])
+            y_s[i, rows] = rows_of(rhs_s, at(f))[rows] - image - local_prior(f, x_s, rows)
+    for g in range(groups):
+        send(1, g)
+    for f, image in zip(inner, images):
+        r_s[f] = rows_of(rhs_s, at(f)) - image - local_prior(f, x_s)
     advance()
 
     for f, image in zip(inner, apply_beam(inner, [r_s[f] for f in inner])):
         u_s[f] = image
     advance()
 
-    arrive(0)
-    for i, f in enumerate(edges):
-        halo = jnp.concatenate([first_s[i, :, 0, :], first_s[i, :, 1, :]], axis=0)
-        r_s[f] = y_s[i] + smooth * halo
-    for i, (f, image) in enumerate(zip(edges, apply_beam(edges, [r_s[f] for f in edges]))):
-        v_s[i] = image + local_prior(f, r_s)
-    send(2)
+    for g in range(groups):
+        arrive(0, g)
+        rows = group(g)
+        for i, f in enumerate(edges):
+            halo = jnp.concatenate([first_s[i, 4 * g:4 * g + 4, b, :] for b in range(2)], axis=0)
+            r_s[f, rows] = y_s[i, rows] + smooth * halo
+        for i, f in enumerate(edges):
+            v_s[i, rows] = edge_beam(f, g, r_s[f, rows]) + local_prior(f, r_s, rows)
+        send(2, g)
     advance()
 
     for f in inner:
@@ -246,17 +330,22 @@
     seen = {f: project(f, u_s[f]) for f in inner}
     advance()
 
-    arrive(1)
+    for g in range(groups):
+        arrive(1, g)
     for i, f in enumerate(edges):
         u_s[f] = v_s[i] - beside(i, smooth * (halo_s[0, i] + smooth * x_s[f]))
-    for f in edges:
-        seen[f] = project(f, u_s[f])
+    edge_seen = {f: [edge_project(f, g, u_s[f, group(g)]) for g in range(groups)] for f in edges}
     norm = jnp.zeros((2 * modes, ell), F32)
     curve, square, cube = norm, norm, norm
-    beam_part = jnp.zeros((modes, width), F32)
+    beam_part = jnp.zeros((2 * modes, width), F32)
+    column_part = jnp.zeros((rank, 128), F32)
     for f in inner + edges:
-        real, imaginary, real_weighted, imaginary_weighted = seen[f]
-        beam_part = beam_part + (real * real_weighted + imaginary * imaginary_weighted)
+        if f in inner:
+            beam_part = beam_part + seen[f][0] * seen[f][1]
+        else:
+            for parts in edge_seen[f]:
+                for real, imaginary, real_weighted, imaginary_weighted in parts:
+                    column_part = column_part + (real * real_weighted + imaginary * imaginary_weighted)
         w_s[f] = local_prior(f, u_s)
         norm = norm + r_s[f] * r_s[f]
         curve = curve + r_s[f] * u_s[f]
@@ -267,7 +356,7 @@
     for i, part in enumerate((norm, curve, square, cube)):
         total = total_of(part)
         if i == 3:
-            total = total + total_of(beam_part)
+            total = total + total_of(beam_part) + jnp.sum(column_part, axis=0, keepdims=True)
         message = jnp.where(lane == i, total, message)
     message_s[0] = message
     early_s[me] = message
@@ -304,26 +393,32 @@
             pltpu.make_async_copy(rows, rows, sem).wait()
 
     share_all(0, early_s, 0)
-    for f in inner + edges:
-        w_s[f] = w_s[f] + back(f, *seen[f][2:])
-
-    arrive(2)
-    cross = jnp.zeros((2 * modes, ell), F32)
+    for f in inner:
+        w_s[f] = w_s[f] + back(f, seen[f][1])
+    for f in edges:
+        for g in range(groups):
+            w_s[f, group(g)] = w_s[f, group(g)] + edge_back(f, g, edge_seen[f][g])
+
+    cross = jnp.zeros((8, ell), F32)
     nexts = []
-    for i, f in enumerate(edges):
-        pull = beside(i, smooth * (halo_s[1, i] - smooth * r_s[f]))
-        nexts.append(pull)
-        cross = cross + pull * u_s[f]
+    for g in range(groups):
+        arrive(2, g)
+        rows = group(g)
+        for i, f in enumerate(edges):
+            pull = beside(i, smooth * (halo_s[1, i, rows] - smooth * r_s[f, rows]))
+            nexts.append((f, rows, pull))
+            cross = cross + pull * u_s[f, rows]
     message = jnp.sum(cross, axis=0, keepdims=True)
     message = sum(message[:, i:i + 128] for i in range(0, ell, 128))
     late_s[my_ma if nf == 2 else me] = message
     message_s[1] = message
     share_all(1, late_s, 1)
-    for f, pull in zip(edges, nexts):
-        w_s[f] = w_s[f] - pull
+    for f, rows, pull in nexts:
+        w_s[f, rows] = w_s[f, rows] - pull
 
     for kind in range(3):
-        sent(kind)
+        for g in range(groups):
+            sent(kind, g)
     landed(early_s, sum_recv.at[0])
     total = jnp.sum(early_s[...], axis=0)
     m0, m1, m2, m3 = (
@@ -336,12 +431,16 @@
     cross_scale = step * step * (2.0 if nf == 2 else 1.0)
     for f in range(freqs):
         x, r, u, w = x_s[f], r_s[f], u_s[f], w_s[f]
-        for b in range(2):
-            rows = slice(b * modes, (b + 1) * modes)
-            sol_s[:, at(f), b, :] = x[rows] + step * r[rows]
-            res_s[:, at(f), b, :] = r[rows] - step * u[rows]
-            sol_move_s[:, at(f), b, :] = (1.0 + growth) * r[rows] - step * u[rows]
-            res_move_s[:, at(f), b, :] = (1.0 + growth) * u[rows] - step * w[rows]
+        for target, value in (
+            (sol_s, x + step * r),
+            (res_s, r - step * u),
+            (sol_move_s, (1.0 + growth) * r - step * u),
+            (res_move_s, (1.0 + growth) * u - step * w),
+        ):
+            for g in range(groups):
+                for b in range(2):
+                    start = 8 * g + 4 * b
+                    target[4 * g:4 * g + 4, at(f), b, :] = value[start:start + 4]
     landed(early_s, sum_send.at[0])
     landed(late_s, sum_send.at[1])
 
@@ -375,7 +474,8 @@
     edge = pltpu.VMEM((sides, modes, 2, ell), F32)
     slab = pltpu.VMEM((freqs, 2 * modes, ell), F32)
     edge_slab = pltpu.VMEM((sides, 2 * modes, ell), F32)
-    half = pltpu.VMEM((freqs, 2 * width, ell), BF16)
+    inner = max(freqs - min(nf - 1, 2), 1)
+    half = pltpu.VMEM((inner, 2 * width, ell), BF16)
     outs = pl.pallas_call(
         functools.partial(kernel, nma, nf),
         out_shape=[field] * 2,
@@ -388,7 +488,8 @@
             pltpu.VMEM((1, ell), F32), pltpu.VMEM((1, ell), F32),
             half, half,
             slab, edge_slab, slab, edge_slab, slab, slab,
-            pltpu.VMEM((freqs, modes, width), F32),
+            pltpu.VMEM((inner, 2 * modes, width), F32),
+            pltpu.VMEM((sides, modes, rank, 128), F32),
             edge,
             pltpu.VMEM((2, sides, 2 * modes, ell), F32),
             field, field,
@@ -397,8 +498,8 @@
             pltpu.VMEM((nma if nf == 2 else nma * nf, 1, 128), F32),
             pltpu.SemaphoreType.DMA((7,)),
             pltpu.SemaphoreType.DMA((freqs,)),
-            pltpu.SemaphoreType.DMA((3, sides)),
-            pltpu.SemaphoreType.DMA((3, sides)),
+            pltpu.SemaphoreType.DMA((3, modes // 4, sides)),
+            pltpu.SemaphoreType.DMA((3, modes // 4, sides)),
             pltpu.SemaphoreType.DMA((2,)),
             pltpu.SemaphoreType.DMA((2,)),
             pltpu.SemaphoreType.REGULAR((max((nma * nf).bit_length() - 2, 1),)),

time: 17.6 us -> 17.2 us (0.977)
  Pallas kernels: 16.8 us -> 16.4 us
    pallas_call x1, Pallas kernels: 16.1 us -> 15.7 us  [shards(): pl.pallas_call(functools.partial(kernel, nma, nf), out_shape=[field] * 2,...]
where the time goes in v2:
time: 17.2 us; the launch traced here: 17.1 us
  Pallas kernels  16.4 us (95%)
  between operations  0.64 us (4%)
    pallas_call x1, Pallas kernels, shards(): pl.pallas_call(functools.partial(kernel, nma, nf), out_shape=[field] * 2,...  15.7 us
    pallas_call x1, Pallas kernels, shards(): pl.pallas_call(write_out, out_shape=[jax.ShapeDtypeStruct(right_side.shap...  0.72 us

profile of v2, /device:TPU:0, one launch (start us, length us, event | category | flops | bytes accessed | tf_op | source)
XLA Modules:
  0.0 17.1 jit_solution(11368635938693934031)
XLA Ops:
  0.6 15.7 %solve.1 = (f32[8,4,2,512]{3,2,1,0:T(2,128)S(1)}, f32[8,4,2,512]{3,2,1,0:T(2,128)S(1)}) custom-call(f32[8,4,2,512]{3,2,1,0:T(2,128)} %rhs_in.1, f32[8,4,2,512]{3,2,1,0:T(2,128)} %x0_in.1, f32[8,4,2,16,512]{4,3,2,1,0:T(8,128)} %beam_in.1, f32[8,4,16]{2,1,0:T(4,128)} %noise_in.1, f32[1,512]{1,0:T(1,128)} %bitcast.2, f32[1,512]{1,0:T(1,128)} %bitcast.3), custom_call_target="tpu_custom_call" | custom-call | tf_op jit(solution)/shard_map/solve/pallas_call | solution.py:479
  16.3 0.7 %write_out.1 = (f32[8,4,2,512]{3,2,1,0:T(2,128)}, f32[8,4,2,512]{3,2,1,0:T(2,128)}) custom-call(f32[8,4,2,512]{3,2,1,0:T(2,128)S(1)} %get-tuple-element.4.sol_in, f32[8,4,2,512]{3,2,1,0:T(2,128)S(1)} %get-tuple-element.5.res_in), custom_call_target="tpu_custom_call" | custom-call | tf_op jit(solution)/shard_map/write_out/pallas_call | solution.py:512

commit v3 on v2

--- a/solution.py
+++ b/solution.py
@@ -54,8 +54,8 @@
     nma, nf, rhs_in, x0_in, beam_in, noise_in, power_in, smooth_in, sol_s, res_s,
     rhs_s, x0_s, edge_s, beam_s, noise_s, power_s, smooth_s,
     high_s, low_s, x_s, y_s, r_s, v_s, u_s, w_s, mask_s, column_s, first_s, halo_s,
-    sol_move_s, res_move_s, message_s, early_s, late_s,
-    in_sem, beam_sem, halo_send, halo_recv, sum_send, sum_recv, word_sem,
+    sol_move_s, res_move_s, pull_s, partner_s, cross_s, message_s, early_s, late_s,
+    in_sem, beam_sem, halo_send, halo_recv, pair_sem, sum_send, sum_recv, word_sem,
 ):
     modes, freqs, _, ell = rhs_in.shape
     rank = beam_in.shape[3]
@@ -65,6 +65,8 @@
     me = my_ma * nf + my_f
     last = freqs - 1
     two_sided = nf > 2
+    paired = nf == 2 and nma % 2 == 0
+    helper = my_ma % 2 == 1
     groups = modes // 4
     edges = [0, last][:min(nf - 1, 2)]
     inner = [f for f in range(freqs) if f not in edges]
@@ -87,7 +89,7 @@
         pltpu.make_async_copy(beam_in.at[:, at(f)], beam_s.at[f], beam_sem.at[f])
         for f in range(freqs)
     ]
-    for copy in edge_copies + [x0_copy] + small + [beam_copies[0], rhs_copy] + beam_copies[1:]:
+    for copy in edge_copies:
         copy.start()
 
     def partners(size, place):
@@ -104,9 +106,15 @@
     def greet(device):
         pl.semaphore_signal(barrier, inc=1, device_id=device, device_id_type=MESH)
 
-    for device in word:
+    greeted = list(word)
+    if paired:
+        greeted.append((my_ma + 1 - 2 * (my_ma % 2), 1 - my_f))
+    for i, device in enumerate(greeted):
         greet(device)
-    expected = len(word)
+        if i == 0:
+            for copy in [x0_copy] + small + [beam_copies[0], rhs_copy] + beam_copies[1:]:
+                copy.start()
+    expected = len(greeted)
     if nf > 2:
         pl.when(my_f > 0)(lambda: greet((my_ma, my_f - 1)))
         pl.when(my_f < nf - 1)(lambda: greet((my_ma, my_f + 1)))
@@ -170,6 +178,21 @@
             near_copy(kind, g).wait_send()
         if two_sided:
             pl.when(has_far)(lambda: far_copy(kind, g).wait_send())
+
+    def cross_copy(g):
+        rows = pl.ds(8 * g, 8)
+        return pltpu.make_async_remote_copy(
+            src_ref=v_s.at[0, rows], dst_ref=cross_s.at[rows],
+            send_sem=pair_sem.at[g], recv_sem=pair_sem.at[groups + g],
+            device_id=(my_ma + 1, 1 - my_f), device_id_type=MESH,
+        )
+
+    def pull_copy():
+        return pltpu.make_async_remote_copy(
+            src_ref=pull_s, dst_ref=partner_s,
+            send_sem=pair_sem.at[2 * groups], recv_sem=pair_sem.at[2 * groups + 1],
+            device_id=(my_ma + 1, my_f), device_id_type=MESH,
+        )
 
     def beside(i, value):
         return jnp.where(has_far, value, 0.0) if i else value
@@ -322,7 +345,13 @@
             r_s[f, rows] = y_s[i, rows] + smooth * halo
         for i, f in enumerate(edges):
             v_s[i, rows] = edge_beam(f, g, r_s[f, rows]) + local_prior(f, r_s, rows)
-        send(2, g)
+        if paired:
+            pl.when(jnp.logical_not(helper))(lambda: cross_copy(g).start())
+        else:
+            send(2, g)
+    if paired:
+        for g in range(groups):
+            send(2, g)
     advance()
 
     for f in inner:
@@ -334,6 +363,9 @@
         arrive(1, g)
     for i, f in enumerate(edges):
         u_s[f] = v_s[i] - beside(i, smooth * (halo_s[0, i] + smooth * x_s[f]))
+    if paired:
+        pull_s[...] = smooth * u_s[0]
+        pl.when(jnp.logical_not(helper))(lambda: pull_copy().start())
     edge_seen = {f: [edge_project(f, g, u_s[f, group(g)]) for g in range(groups)] for f in edges}
     norm = jnp.zeros((2 * modes, ell), F32)
     curve, square, cube = norm, norm, norm
@@ -358,14 +390,15 @@
         if i == 3:
             total = total + total_of(beam_part) + jnp.sum(column_part, axis=0, keepdims=True)
         message = jnp.where(lane == i, total, message)
+    if paired:
+        message = jnp.where(lane == 4 + my_f, total_of(smooth * r_s[0] * pull_s[...]), message)
     message_s[0] = message
     early_s[me] = message
 
     while steps:
         advance()
 
-    def share(source, target, turn, offset):
-        slot = my_ma if turn and nf == 2 else me
+    def share(source, target, slot, turn, offset):
         pltpu.make_async_remote_copy(
             src_ref=message_s.at[source], dst_ref=target.at[slot],
             send_sem=sum_send.at[turn], recv_sem=sum_recv.at[turn],
@@ -373,62 +406,93 @@
             device_id_type=MESH,
         ).start()
 
-    def share_all(source, target, turn):
-        stride = nf if turn and nf == 2 else 1
+    def share_all(source, target, slot, turn, stride):
         if n > 64:
             def body(i, carry):
-                share(source, target, turn, i * stride)
+                share(source, target, slot, turn, i * stride)
                 return carry
 
             lax.fori_loop(1, n // stride, body, 0)
         else:
             offsets = range(stride, n, stride)
-            for offset in sorted(offsets, key=lambda o: abs(2 * (o // nf) - nma)):
-                share(source, target, turn, offset)
-
-    def landed(target, sem):
-        count_in = target.shape[0] - 1
-        if count_in:
-            rows = target.at[pl.ds(0, count_in)]
+            for offset in sorted(offsets, key=lambda o: abs(2 * (o // nf) - nma) - 4 * (o // nf % 2)):
+                share(source, target, slot, turn, offset)
+
+    def landed(target, sem, rows):
+        if rows:
+            rows = target.at[pl.ds(0, rows)]
             pltpu.make_async_copy(rows, rows, sem).wait()
 
-    share_all(0, early_s, 0)
+    def lanes_of(x):
+        x = jnp.sum(x, axis=0, keepdims=True)
+        return sum(x[:, i:i + 128] for i in range(0, ell, 128))
+
+    share_all(0, early_s, me, 0, 1)
     for f in inner:
         w_s[f] = w_s[f] + back(f, seen[f][1])
     for f in edges:
         for g in range(groups):
             w_s[f, group(g)] = w_s[f, group(g)] + edge_back(f, g, edge_seen[f][g])
 
-    cross = jnp.zeros((8, ell), F32)
-    nexts = []
-    for g in range(groups):
-        arrive(2, g)
-        rows = group(g)
-        for i, f in enumerate(edges):
-            pull = beside(i, smooth * (halo_s[1, i, rows] - smooth * r_s[f, rows]))
-            nexts.append((f, rows, pull))
-            cross = cross + pull * u_s[f, rows]
-    message = jnp.sum(cross, axis=0, keepdims=True)
-    message = sum(message[:, i:i + 128] for i in range(0, ell, 128))
-    late_s[my_ma if nf == 2 else me] = message
-    message_s[1] = message
-    share_all(1, late_s, 1)
-    for f, rows, pull in nexts:
-        w_s[f, rows] = w_s[f, rows] - pull
+    late_rows = late_s.shape[0]
+    if paired:
+        @pl.when(helper)
+        def _():
+            cross = jnp.zeros((8, ell), F32)
+            for g in range(groups):
+                arrive(2, g)
+                cross = cross + pull_s[group(g)] * halo_s[1, 0, group(g)]
+            pull_copy().wait_recv()
+            for g in range(groups):
+                cross_copy(g).wait_recv()
+                cross = cross + partner_s[group(g)] * cross_s[group(g)]
+            message = lanes_of(cross)
+            late_s[my_ma // 2] = message
+            message_s[1] = message
+            share_all(1, late_s, my_ma // 2, 1, nf)
+
+        @pl.when(jnp.logical_not(helper))
+        def _():
+            for g in range(groups):
+                arrive(2, g)
+            pull_copy().wait_send()
+            for g in range(groups):
+                cross_copy(g).wait_send()
+
+        w_s[0] = w_s[0] - smooth * (halo_s[1, 0] - smooth * r_s[0])
+    else:
+        cross = jnp.zeros((8, ell), F32)
+        nexts = []
+        for g in range(groups):
+            arrive(2, g)
+            rows = group(g)
+            for i, f in enumerate(edges):
+                pull = beside(i, smooth * (halo_s[1, i, rows] - smooth * r_s[f, rows]))
+                nexts.append((f, rows, pull))
+                cross = cross + pull * u_s[f, rows]
+        message = lanes_of(cross)
+        late_s[me] = message
+        message_s[1] = message
+        share_all(1, late_s, me, 1, 1)
+        for f, rows, pull in nexts:
+            w_s[f, rows] = w_s[f, rows] - pull
 
     for kind in range(3):
         for g in range(groups):
             sent(kind, g)
-    landed(early_s, sum_recv.at[0])
+    landed(early_s, sum_recv.at[0], n - 1)
     total = jnp.sum(early_s[...], axis=0)
-    m0, m1, m2, m3 = (
-        jnp.sum(jnp.where(lane == i, total, 0.0), axis=1, keepdims=True) for i in range(4)
+    m0, m1, m2, m3, known = (
+        jnp.sum(jnp.where(lane == i, total, 0.0), axis=1, keepdims=True)
+        for i in (0, 1, 2, 3, 4 + my_f)
     )
+    if paired:
+        m3 = m3 + 2.0 * known
     step = m0 / m1
     norm_next = step * (step * m2 - m1)
     growth = norm_next / m0
     curve_part = m1 - 2.0 * step * m2 + step * step * m3 - growth * norm_next / step
-    cross_scale = step * step * (2.0 if nf == 2 else 1.0)
+    cross_scale = step * step * (2.0 if paired else 1.0)
     for f in range(freqs):
         x, r, u, w = x_s[f], r_s[f], u_s[f], w_s[f]
         for target, value in (
@@ -441,10 +505,18 @@
                 for b in range(2):
                     start = 8 * g + 4 * b
                     target[4 * g:4 * g + 4, at(f), b, :] = value[start:start + 4]
-    landed(early_s, sum_send.at[0])
-    landed(late_s, sum_send.at[1])
-
-    landed(late_s, sum_recv.at[1])
+    landed(early_s, sum_send.at[0], n - 1)
+    if paired:
+        @pl.when(helper)
+        def _():
+            rows = early_s.at[pl.ds(0, nma - 1)]
+            pltpu.make_async_copy(rows, rows, sum_send.at[1]).wait()
+            landed(late_s, sum_recv.at[1], late_rows - 1)
+
+        pl.when(jnp.logical_not(helper))(lambda: landed(late_s, sum_recv.at[1], late_rows))
+    else:
+        landed(late_s, sum_send.at[1], late_rows - 1)
+        landed(late_s, sum_recv.at[1], late_rows - 1)
     crossed = jnp.sum(jnp.sum(late_s[...], axis=0), axis=1, keepdims=True)
     step_next = norm_next / (curve_part - cross_scale * crossed)
     sol_s[...] = sol_s[...] + step_next * sol_move_s[...]
@@ -493,13 +565,16 @@
             edge,
             pltpu.VMEM((2, sides, 2 * modes, ell), F32),
             field, field,
+            pltpu.VMEM((2 * modes, ell), F32), pltpu.VMEM((2 * modes, ell), F32),
+            pltpu.VMEM((2 * modes, ell), F32),
             pltpu.VMEM((2, 1, 128), F32),
             pltpu.VMEM((nma * nf, 1, 128), F32),
-            pltpu.VMEM((nma if nf == 2 else nma * nf, 1, 128), F32),
+            pltpu.VMEM((nma // 2 if nf == 2 and nma % 2 == 0 else nma * nf, 1, 128), F32),
             pltpu.SemaphoreType.DMA((7,)),
             pltpu.SemaphoreType.DMA((freqs,)),
             pltpu.SemaphoreType.DMA((3, modes // 4, sides)),
             pltpu.SemaphoreType.DMA((3, modes // 4, sides)),
+            pltpu.SemaphoreType.DMA((2 * (modes // 4) + 2,)),
             pltpu.SemaphoreType.DMA((2,)),
             pltpu.SemaphoreType.DMA((2,)),
             pltpu.SemaphoreType.REGULAR((max((nma * nf).bit_length() - 2, 1),)),

time: 17.2 us -> 16.4 us (0.953)
  Pallas kernels: 16.4 us -> 15.6 us
    pallas_call x1, Pallas kernels: 15.7 us -> 14.9 us  [shards(): pl.pallas_call(functools.partial(kernel, nma, nf), out_shape=[field] * 2,...]
where the time goes in v3:
time: 16.4 us; the launch traced here: 16.3 us
  Pallas kernels  15.6 us (95%)
  between operations  0.64 us (4%)
    pallas_call x1, Pallas kernels, shards(): pl.pallas_call(functools.partial(kernel, nma, nf), out_shape=[field] * 2,...  14.9 us
    pallas_call x1, Pallas kernels, shards(): pl.pallas_call(write_out, out_shape=[jax.ShapeDtypeStruct(right_side.shap...  0.72 us

profile of v3, /device:TPU:0, one launch (start us, length us, event | category | flops | bytes accessed | tf_op | source)
XLA Modules:
  0.0 16.3 jit_solution(10229567558393174121)
XLA Ops:
  0.6 14.9 %solve.1 = (f32[8,4,2,512]{3,2,1,0:T(2,128)S(1)}, f32[8,4,2,512]{3,2,1,0:T(2,128)S(1)}) custom-call(f32[8,4,2,512]{3,2,1,0:T(2,128)} %rhs_in.1, f32[8,4,2,512]{3,2,1,0:T(2,128)} %x0_in.1, f32[8,4,2,16,512]{4,3,2,1,0:T(8,128)} %beam_in.1, f32[8,4,16]{2,1,0:T(4,128)} %noise_in.1, f32[1,512]{1,0:T(1,128)} %bitcast.2, f32[1,512]{1,0:T(1,128)} %bitcast.3), custom_call_target="tpu_custom_call" | custom-call | tf_op jit(solution)/shard_map/solve/pallas_call | solution.py:551
  15.5 0.7 %write_out.1 = (f32[8,4,2,512]{3,2,1,0:T(2,128)}, f32[8,4,2,512]{3,2,1,0:T(2,128)}) custom-call(f32[8,4,2,512]{3,2,1,0:T(2,128)S(1)} %get-tuple-element.4.sol_in, f32[8,4,2,512]{3,2,1,0:T(2,128)S(1)} %get-tuple-element.5.res_in), custom_call_target="tpu_custom_call" | custom-call | tf_op jit(solution)/shard_map/write_out/pallas_call | solution.py:587

commit v4 on v3

--- a/solution.py
+++ b/solution.py
@@ -55,7 +55,7 @@
     rhs_s, x0_s, edge_s, beam_s, noise_s, power_s, smooth_s,
     high_s, low_s, x_s, y_s, r_s, v_s, u_s, w_s, mask_s, column_s, first_s, halo_s,
     sol_move_s, res_move_s, pull_s, partner_s, cross_s, message_s, early_s, late_s,
-    in_sem, beam_sem, halo_send, halo_recv, pair_sem, sum_send, sum_recv, word_sem,
+    halo_recv, pair_sem, sum_recv, word_sem, in_sem, beam_sem, halo_send, sum_send,
 ):
     modes, freqs, _, ell = rhs_in.shape
     rank = beam_in.shape[3]
@@ -70,6 +70,10 @@
     groups = modes // 4
     edges = [0, last][:min(nf - 1, 2)]
     inner = [f for f in range(freqs) if f not in edges]
+    beside_edge = [f for f in inner if f - 1 in edges or f + 1 in edges]
+    apart = [f for f in inner if f not in beside_edge]
+    vector = edges + inner[:max(freqs // 2 - len(edges), 0)]
+    matrix = [f for f in range(freqs) if f not in vector]
 
     def at(g):
         return jnp.where(my_f == 0, last - g, g)
@@ -92,13 +96,26 @@
     for copy in edge_copies:
         copy.start()
 
-    def partners(size, place):
-        distances = [1 << bit for bit in range(size.bit_length() - 1)]
-        return [place + d * (1 - 2 * (place // d % 2)) for d in distances]
-
-    word = [(my_ma, other) for other in partners(nf, my_f)]
-    word += [(other, my_f) for other in partners(nma, my_ma)]
-    words = max(len(word) - 1, 0)
+    def flip(bit):
+        d = 1 << (bit if bit < freq_bits else bit - freq_bits)
+        place = my_f if bit < freq_bits else my_ma
+        return d * (1 - 2 * (place // d % 2))
+
+    def partner(bits):
+        return (
+            my_ma + sum(flip(bit) for bit in bits if bit >= freq_bits),
+            my_f + sum(flip(bit) for bit in bits if bit < freq_bits),
+        )
+
+    freq_bits = nf.bit_length() - 1
+    bits = freq_bits + nma.bit_length() - 1
+    close = min(bits, 3)
+    greeted = [
+        partner([bit for bit in range(close) if mask >> bit & 1]) for mask in range(1, 1 << close)
+    ]
+    word = [partner([bit]) for bit in range(close, bits)]
+    greeted += word
+    words = len(word)
     barrier = pltpu.get_barrier_semaphore()
     near = jnp.where(my_f == 0, 1, my_f - 1)
     has_far = (my_f > 0) & (my_f < nf - 1)
@@ -106,13 +123,11 @@
     def greet(device):
         pl.semaphore_signal(barrier, inc=1, device_id=device, device_id_type=MESH)
 
-    greeted = list(word)
-    if paired:
-        greeted.append((my_ma + 1 - 2 * (my_ma % 2), 1 - my_f))
     for i, device in enumerate(greeted):
         greet(device)
         if i == 0:
-            for copy in [x0_copy] + small + [beam_copies[0], rhs_copy] + beam_copies[1:]:
+            others = [beam_copies[f] for f in edges] + [rhs_copy] + [beam_copies[f] for f in inner]
+            for copy in [x0_copy] + small + others:
                 copy.start()
     expected = len(greeted)
     if nf > 2:
@@ -229,7 +244,7 @@
     row = lax.broadcasted_iota(jnp.int32, (2 * modes, width), 0)
     own = lax.broadcasted_iota(jnp.int32, (2 * modes, width), 1) // rank == row // 8 * 4 + row % 4
     sign = jnp.where(row % 8 < 4, 1.0, -1.0)
-    for i, f in enumerate(inner):
+    for i, f in enumerate(matrix):
         levels = noise_s[:, at(f), :]
         levels = jnp.concatenate(
             [levels[4 * g:4 * g + 4] for g in range(groups) for _ in range(2)], axis=0
@@ -239,7 +254,7 @@
         lax.broadcasted_iota(jnp.int32, (rank, rank), 0)
         == lax.broadcasted_iota(jnp.int32, (rank, rank), 1)
     )
-    for i, f in enumerate(edges):
+    for i, f in enumerate(vector):
         levels = noise_s[:, at(f), :]
         for m in range(modes):
             column = jnp.sum(jnp.where(unit, levels[m:m + 1], 0.0), axis=1, keepdims=True)
@@ -248,31 +263,27 @@
     def swapped(x):
         return jnp.concatenate([pltpu.roll(x[group(g)], 4, 0) for g in range(groups)], axis=0)
 
-    def project(f, field):
-        i = inner.index(f)
+    def matrix_project(f, field):
+        i = matrix.index(f)
         seen = times(field, high_s[i], low_s[i], True)
         parts = seen[:, :width] + sign * swapped(seen[:, width:])
         return parts, mask_s[i] * parts
 
-    def back(f, weighted):
-        i = inner.index(f)
-        weighted = jnp.concatenate([weighted, -sign * swapped(weighted)], axis=1)
+    def matrix_back(f, seen):
+        i = matrix.index(f)
+        weighted = jnp.concatenate([seen[1], -sign * swapped(seen[1])], axis=1)
         return times(weighted, high_s[i], low_s[i], False)
-
-    def apply_beam(fs, fields):
-        parts = [project(f, field) for f, field in zip(fs, fields)]
-        return [back(f, part[1]) for f, part in zip(fs, parts)]
 
     def wide(x):
         return jnp.concatenate([x] * (ell // 128), axis=1)
 
-    def edge_project(f, g, field):
+    def group_project(f, g, field):
         parts = []
         for j in range(4):
             m = 4 * g + j
             real_beam, imaginary_beam = beam_s[f, m, 0], beam_s[f, m, 1]
             real_field, imaginary_field = field[j:j + 1], field[4 + j:5 + j]
-            levels = column_s[edges.index(f), m]
+            levels = column_s[vector.index(f), m]
             real = jnp.sum(
                 real_beam * real_field + imaginary_beam * imaginary_field, axis=1, keepdims=True
             )
@@ -282,7 +293,7 @@
             parts.append((real, imaginary, levels * real, levels * imaginary))
         return parts
 
-    def edge_back(f, g, parts):
+    def group_back(f, g, parts):
         reals, imaginaries = [], []
         for j, (_, _, real, imaginary) in enumerate(parts):
             m = 4 * g + j
@@ -295,8 +306,23 @@
                 found.append(sum(value[k:k + 8] for k in range(0, rank, 8)))
         return folded(reals + imaginaries)
 
-    def edge_beam(f, g, field):
-        return edge_back(f, g, edge_project(f, g, field))
+    def group_beam(f, g, field):
+        return group_back(f, g, group_project(f, g, field))
+
+    def project(f, ref):
+        if f in matrix:
+            return matrix_project(f, ref[f])
+        return [group_project(f, g, ref[f, group(g)]) for g in range(groups)]
+
+    def back(f, seen):
+        if f in matrix:
+            return matrix_back(f, seen)
+        return jnp.concatenate([group_back(f, g, seen[g]) for g in range(groups)], axis=0)
+
+    def apply_beam(fs, ref):
+        fs = [f for f in fs if f in matrix] + [f for f in fs if f in vector]
+        seen = [project(f, ref) for f in fs]
+        return {f: back(f, found) for f, found in zip(fs, seen)}
 
     def count(f):
         value = float(f > 0) + float(f < last) + float(nf > 1 and f == 0)
@@ -312,29 +338,30 @@
             value = value - ref[f + 1, rows]
         return power * ref[f, rows] + smooth * value
 
-    for copy in beam_copies:
-        copy.wait()
+    for f in edges:
+        beam_copies[f].wait()
     rhs_copy.wait()
-    for i, f in enumerate(inner):
+    for i, f in enumerate(edges):
+        for g in range(groups):
+            rows = group(g)
+            image = group_beam(f, g, x_s[f, rows])
+            y_s[i, rows] = rows_of(rhs_s, at(f))[rows] - image - local_prior(f, x_s, rows)
+    for g in range(groups):
+        send(1, g)
+
+    for f in inner:
+        beam_copies[f].wait()
+    for i, f in enumerate(matrix):
         for a in range(2):
             rows = slice(a * width, (a + 1) * width)
             high, low = split(beam_s[f, :, a].reshape(width, ell))
             high_s[i, rows] = high
             low_s[i, rows] = low
-    images = apply_beam(inner, [x_s[f] for f in inner])
-    for i, f in enumerate(edges):
-        for g in range(groups):
-            rows = group(g)
-            image = edge_beam(f, g, x_s[f, rows])
-            y_s[i, rows] = rows_of(rhs_s, at(f))[rows] - image - local_prior(f, x_s, rows)
-    for g in range(groups):
-        send(1, g)
-    for f, image in zip(inner, images):
+    for f, image in apply_beam(inner, x_s).items():
         r_s[f] = rows_of(rhs_s, at(f)) - image - local_prior(f, x_s)
-    advance()
-
-    for f, image in zip(inner, apply_beam(inner, [r_s[f] for f in inner])):
-        u_s[f] = image
+    for f, image in apply_beam(inner, r_s).items():
+        u_s[f] = image + local_prior(f, r_s) if f in apart else image
+    seen = {f: project(f, u_s) for f in apart}
     advance()
 
     for g in range(groups):
@@ -344,7 +371,7 @@
             halo = jnp.concatenate([first_s[i, 4 * g:4 * g + 4, b, :] for b in range(2)], axis=0)
             r_s[f, rows] = y_s[i, rows] + smooth * halo
         for i, f in enumerate(edges):
-            v_s[i, rows] = edge_beam(f, g, r_s[f, rows]) + local_prior(f, r_s, rows)
+            v_s[i, rows] = group_beam(f, g, r_s[f, rows]) + local_prior(f, r_s, rows)
         if paired:
             pl.when(jnp.logical_not(helper))(lambda: cross_copy(g).start())
         else:
@@ -352,12 +379,10 @@
     if paired:
         for g in range(groups):
             send(2, g)
-    advance()
-
-    for f in inner:
+
+    for f in beside_edge:
         u_s[f] = u_s[f] + local_prior(f, r_s)
-    seen = {f: project(f, u_s[f]) for f in inner}
-    advance()
+    seen |= {f: project(f, u_s) for f in beside_edge}
 
     for g in range(groups):
         arrive(1, g)
@@ -366,16 +391,16 @@
     if paired:
         pull_s[...] = smooth * u_s[0]
         pl.when(jnp.logical_not(helper))(lambda: pull_copy().start())
-    edge_seen = {f: [edge_project(f, g, u_s[f, group(g)]) for g in range(groups)] for f in edges}
+    seen |= {f: project(f, u_s) for f in edges}
     norm = jnp.zeros((2 * modes, ell), F32)
     curve, square, cube = norm, norm, norm
     beam_part = jnp.zeros((2 * modes, width), F32)
     column_part = jnp.zeros((rank, 128), F32)
     for f in inner + edges:
-        if f in inner:
+        if f in matrix:
             beam_part = beam_part + seen[f][0] * seen[f][1]
         else:
-            for parts in edge_seen[f]:
+            for parts in seen[f]:
                 for real, imaginary, real_weighted, imaginary_weighted in parts:
                     column_part = column_part + (real * real_weighted + imaginary * imaginary_weighted)
         w_s[f] = local_prior(f, u_s)
@@ -428,11 +453,8 @@
         return sum(x[:, i:i + 128] for i in range(0, ell, 128))
 
     share_all(0, early_s, me, 0, 1)
-    for f in inner:
-        w_s[f] = w_s[f] + back(f, seen[f][1])
-    for f in edges:
-        for g in range(groups):
-            w_s[f, group(g)] = w_s[f, group(g)] + edge_back(f, g, edge_seen[f][g])
+    for f in matrix + vector:
+        w_s[f] = w_s[f] + back(f, seen[f])
 
     late_rows = late_s.shape[0]
     if paired:
@@ -523,6 +545,15 @@
     res_s[...] = res_s[...] - step_next * res_move_s[...]
 
 
+def scoped_kernel(nma, nf, sides, *refs):
+    modes, freqs = refs[0].shape[:2]
+    dma = pltpu.SemaphoreType.DMA
+    pl.run_scoped(
+        functools.partial(kernel, nma, nf, *refs),
+        dma((7,)), dma((freqs,)), dma((3, modes // 4, sides)), dma((2,)),
+    )
+
+
 def write_out(sol_in, res_in, sol_out, res_out, sem):
     copies = [
         pltpu.make_async_copy(sol_in, sol_out, sem.at[0]),
@@ -546,10 +577,11 @@
     edge = pltpu.VMEM((sides, modes, 2, ell), F32)
     slab = pltpu.VMEM((freqs, 2 * modes, ell), F32)
     edge_slab = pltpu.VMEM((sides, 2 * modes, ell), F32)
-    inner = max(freqs - min(nf - 1, 2), 1)
-    half = pltpu.VMEM((inner, 2 * width, ell), BF16)
+    vector = max(min(nf - 1, 2), freqs // 2)
+    matrix = max(freqs - vector, 1)
+    half = pltpu.VMEM((matrix, 2 * width, ell), BF16)
     outs = pl.pallas_call(
-        functools.partial(kernel, nma, nf),
+        functools.partial(scoped_kernel, nma, nf, sides),
         out_shape=[field] * 2,
         in_specs=[any_spec] * 6,
         out_specs=[vmem_spec] * 2,
@@ -560,8 +592,8 @@
             pltpu.VMEM((1, ell), F32), pltpu.VMEM((1, ell), F32),
             half, half,
             slab, edge_slab, slab, edge_slab, slab, slab,
-            pltpu.VMEM((inner, 2 * modes, width), F32),
-            pltpu.VMEM((sides, modes, rank, 128), F32),
+            pltpu.VMEM((matrix, 2 * modes, width), F32),
+            pltpu.VMEM((vector, modes, rank, 128), F32),
             edge,
             pltpu.VMEM((2, sides, 2 * modes, ell), F32),
             field, field,
@@ -570,14 +602,10 @@
             pltpu.VMEM((2, 1, 128), F32),
             pltpu.VMEM((nma * nf, 1, 128), F32),
             pltpu.VMEM((nma // 2 if nf == 2 and nma % 2 == 0 else nma * nf, 1, 128), F32),
-            pltpu.SemaphoreType.DMA((7,)),
-            pltpu.SemaphoreType.DMA((freqs,)),
-            pltpu.SemaphoreType.DMA((3, modes // 4, sides)),
             pltpu.SemaphoreType.DMA((3, modes // 4, sides)),
             pltpu.SemaphoreType.DMA((2 * (modes // 4) + 2,)),
             pltpu.SemaphoreType.DMA((2,)),
-            pltpu.SemaphoreType.DMA((2,)),
-            pltpu.SemaphoreType.REGULAR((max((nma * nf).bit_length() - 2, 1),)),
+            pltpu.SemaphoreType.REGULAR((max((nma * nf).bit_length() - 4, 1),)),
         ],
         compiler_params=pltpu.CompilerParams(
             collective_id=0, has_side_effects=True, vmem_limit_bytes=67043328 - 2 * right_side.size * 4

time: 16.4 us -> 16.4 us (level)
  no operation moved by 1% of the time
where the time goes in v4:
time: 16.4 us; the launch traced here: 16.2 us
  Pallas kernels  15.6 us (95%)
  between operations  0.64 us (4%)
    pallas_call x1, Pallas kernels, shards(): pl.pallas_call(functools.partial(scoped_kernel, nma, nf, sides), out_shap...  14.9 us
    pallas_call x1, Pallas kernels, shards(): pl.pallas_call(write_out, out_shape=[jax.ShapeDtypeStruct(right_side.shap...  0.72 us

profile of v4, /device:TPU:0, one launch (start us, length us, event | category | flops | bytes accessed | tf_op | source)
XLA Modules:
  0.0 16.2 jit_solution(17896404635812306190)
XLA Ops:
  0.6 14.9 %solve.1 = (f32[8,4,2,512]{3,2,1,0:T(2,128)S(1)}, f32[8,4,2,512]{3,2,1,0:T(2,128)S(1)}) custom-call(f32[8,4,2,512]{3,2,1,0:T(2,128)} %refs_0_.1, f32[8,4,2,512]{3,2,1,0:T(2,128)} %refs_1_.1, f32[8,4,2,16,512]{4,3,2,1,0:T(8,128)} %refs_2_.1, f32[8,4,16]{2,1,0:T(4,128)} %refs_3_.1, f32[1,512]{1,0:T(1,128)} %bitcast.2, f32[1,512]{1,0:T(1,128)} %bitcast.3), custom_call_target="tpu_custom_call" | custom-call | tf_op jit(solution)/shard_map/solve/pallas_call | solution.py:583
  15.5 0.7 %write_out.1 = (f32[8,4,2,512]{3,2,1,0:T(2,128)}, f32[8,4,2,512]{3,2,1,0:T(2,128)}) custom-call(f32[8,4,2,512]{3,2,1,0:T(2,128)S(1)} %get-tuple-element.4.sol_in, f32[8,4,2,512]{3,2,1,0:T(2,128)S(1)} %get-tuple-element.5.res_in), custom_call_target="tpu_custom_call" | custom-call | tf_op jit(solution)/shard_map/write_out/pallas_call | solution.py:615

commit v5 on v4

--- a/solution.py
+++ b/solution.py
@@ -423,25 +423,25 @@
     while steps:
         advance()
 
-    def share(source, target, slot, turn, offset):
+    def share(source, target, slot, turn, device):
         pltpu.make_async_remote_copy(
             src_ref=message_s.at[source], dst_ref=target.at[slot],
             send_sem=sum_send.at[turn], recv_sem=sum_recv.at[turn],
-            device_id=(lax.rem(my_ma + offset // nf, nma), lax.rem(my_f + offset % nf, nf)),
-            device_id_type=MESH,
+            device_id=device, device_id_type=MESH,
         ).start()
 
     def share_all(source, target, slot, turn, stride):
         if n > 64:
             def body(i, carry):
-                share(source, target, slot, turn, i * stride)
+                ma, f = my_ma + i * stride // nf, my_f + i * stride % nf
+                share(source, target, slot, turn, (lax.rem(ma, nma), lax.rem(f, nf)))
                 return carry
 
             lax.fori_loop(1, n // stride, body, 0)
         else:
-            offsets = range(stride, n, stride)
-            for offset in sorted(offsets, key=lambda o: abs(2 * (o // nf) - nma) - 4 * (o // nf % 2)):
-                share(source, target, slot, turn, offset)
+            for mask in sorted(range(stride, n, stride), key=lambda m: (-(m // nf // 2), m)):
+                device = partner([bit for bit in range(bits) if mask >> bit & 1])
+                share(source, target, slot, turn, device)
 
     def landed(target, sem, rows):
         if rows:

time: 16.4 us -> 16.3 us (level)
  no operation moved by 1% of the time
where the time goes in v5:
time: 16.3 us; the launch traced here: 16.2 us
  Pallas kernels  15.5 us (95%)
  between operations  0.64 us (4%)
    pallas_call x1, Pallas kernels, shards(): pl.pallas_call(functools.partial(scoped_kernel, nma, nf, sides), out_shap...  14.8 us
    pallas_call x1, Pallas kernels, shards(): pl.pallas_call(write_out, out_shape=[jax.ShapeDtypeStruct(right_side.shap...  0.72 us

profile of v5, /device:TPU:0, one launch (start us, length us, event | category | flops | bytes accessed | tf_op | source)
XLA Modules:
  0.0 16.2 jit_solution(14623967204677428569)
XLA Ops:
  0.6 14.8 %solve.1 = (f32[8,4,2,512]{3,2,1,0:T(2,128)S(1)}, f32[8,4,2,512]{3,2,1,0:T(2,128)S(1)}) custom-call(f32[8,4,2,512]{3,2,1,0:T(2,128)} %refs_0_.1, f32[8,4,2,512]{3,2,1,0:T(2,128)} %refs_1_.1, f32[8,4,2,16,512]{4,3,2,1,0:T(8,128)} %refs_2_.1, f32[8,4,16]{2,1,0:T(4,128)} %refs_3_.1, f32[1,512]{1,0:T(1,128)} %bitcast.2, f32[1,512]{1,0:T(1,128)} %bitcast.3), custom_call_target="tpu_custom_call" | custom-call | tf_op jit(solution)/shard_map/solve/pallas_call | solution.py:583
  15.5 0.7 %write_out.1 = (f32[8,4,2,512]{3,2,1,0:T(2,128)}, f32[8,4,2,512]{3,2,1,0:T(2,128)}) custom-call(f32[8,4,2,512]{3,2,1,0:T(2,128)S(1)} %get-tuple-element.4.sol_in, f32[8,4,2,512]{3,2,1,0:T(2,128)S(1)} %get-tuple-element.5.res_in), custom_call_target="tpu_custom_call" | custom-call | tf_op jit(solution)/shard_map/write_out/pallas_call | solution.py:615

commit v6 on v5

--- a/solution.py
+++ b/solution.py
@@ -54,8 +54,10 @@
     nma, nf, rhs_in, x0_in, beam_in, noise_in, power_in, smooth_in, sol_s, res_s,
     rhs_s, x0_s, edge_s, beam_s, noise_s, power_s, smooth_s,
     high_s, low_s, x_s, y_s, r_s, v_s, u_s, w_s, mask_s, column_s, first_s, halo_s,
-    sol_move_s, res_move_s, pull_s, partner_s, cross_s, message_s, early_s, late_s,
-    halo_recv, pair_sem, sum_recv, word_sem, in_sem, beam_sem, halo_send, sum_send,
+    sol_move_s, res_move_s, pull_s, partner_s, cross_s,
+    lent_beam_s, lent_column_s, lent_y_s, lent_r_s, lent_first_s, lent_v_s,
+    message_s, early_s, late_s,
+    halo_recv, pair_recv, sum_recv, word_sem, in_sem, beam_sem, halo_send, pair_send, sum_send,
 ):
     modes, freqs, _, ell = rhs_in.shape
     rank = beam_in.shape[3]
@@ -65,7 +67,7 @@
     me = my_ma * nf + my_f
     last = freqs - 1
     two_sided = nf > 2
-    paired = nf == 2 and nma % 2 == 0
+    paired = nf == 2 and nma % 2 == 0 and freqs > 1
     helper = my_ma % 2 == 1
     groups = modes // 4
     edges = [0, last][:min(nf - 1, 2)]
@@ -194,20 +196,33 @@
         if two_sided:
             pl.when(has_far)(lambda: far_copy(kind, g).wait_send())
 
+    def pair_copy(k, source, target, ma, f):
+        return pltpu.make_async_remote_copy(
+            src_ref=source, dst_ref=target, send_sem=pair_send.at[k], recv_sem=pair_recv.at[k],
+            device_id=(ma, f), device_id_type=MESH,
+        )
+
+    def lend(k):
+        source = (lambda: beam_s.at[0], lambda: column_s.at[0], lambda: y_s.at[0], lambda: r_s.at[1])[k]
+        target = (lent_beam_s, lent_column_s, lent_y_s, lent_r_s)[k]
+        return pair_copy(k, source(), target, my_ma + 1, my_f)
+
+    def pull_copy():
+        return pair_copy(4, pull_s, partner_s, my_ma + 1, my_f)
+
+    def first_copy(g):
+        rows = pl.ds(4 * g, 4)
+        return pair_copy(5 + g, edge_s.at[0, rows], lent_first_s.at[rows], my_ma + 1, 1 - my_f)
+
     def cross_copy(g):
         rows = pl.ds(8 * g, 8)
-        return pltpu.make_async_remote_copy(
-            src_ref=v_s.at[0, rows], dst_ref=cross_s.at[rows],
-            send_sem=pair_sem.at[g], recv_sem=pair_sem.at[groups + g],
-            device_id=(my_ma + 1, 1 - my_f), device_id_type=MESH,
-        )
-
-    def pull_copy():
-        return pltpu.make_async_remote_copy(
-            src_ref=pull_s, dst_ref=partner_s,
-            send_sem=pair_sem.at[2 * groups], recv_sem=pair_sem.at[2 * groups + 1],
-            device_id=(my_ma + 1, my_f), device_id_type=MESH,
-        )
+        return pair_copy(5 + groups + g, lent_v_s.at[rows], cross_s.at[rows], my_ma, 1 - my_f)
+
+    def even_only(copies):
+        @pl.when(jnp.logical_not(helper))
+        def _():
+            for copy in copies:
+                copy.start()
 
     def beside(i, value):
         return jnp.where(has_far, value, 0.0) if i else value
@@ -223,6 +238,8 @@
     pl.semaphore_wait(barrier, expected)
     for g in range(groups):
         send(0, g)
+    if paired:
+        even_only([first_copy(g) for g in range(groups)])
     advance()
 
     x0_copy.wait()
@@ -277,13 +294,19 @@
     def wide(x):
         return jnp.concatenate([x] * (ell // 128), axis=1)
 
-    def group_project(f, g, field):
+    def owned(f):
+        return (lambda m, a: beam_s[f, m, a]), (lambda m: column_s[vector.index(f), m])
+
+    lent = (lambda m, a: lent_beam_s[m, a]), (lambda m: lent_column_s[m])
+
+    def group_project(source, g, field):
+        beam_of, column_of = source
         parts = []
         for j in range(4):
             m = 4 * g + j
-            real_beam, imaginary_beam = beam_s[f, m, 0], beam_s[f, m, 1]
+            real_beam, imaginary_beam = beam_of(m, 0), beam_of(m, 1)
             real_field, imaginary_field = field[j:j + 1], field[4 + j:5 + j]
-            levels = column_s[vector.index(f), m]
+            levels = column_of(m)
             real = jnp.sum(
                 real_beam * real_field + imaginary_beam * imaginary_field, axis=1, keepdims=True
             )
@@ -293,12 +316,13 @@
             parts.append((real, imaginary, levels * real, levels * imaginary))
         return parts
 
-    def group_back(f, g, parts):
+    def group_back(source, g, parts):
+        beam_of, _ = source
         reals, imaginaries = [], []
         for j, (_, _, real, imaginary) in enumerate(parts):
             m = 4 * g + j
             real, imaginary = wide(real), wide(imaginary)
-            real_beam, imaginary_beam = beam_s[f, m, 0], beam_s[f, m, 1]
+            real_beam, imaginary_beam = beam_of(m, 0), beam_of(m, 1)
             for found, value in (
                 (reals, real_beam * real - imaginary_beam * imaginary),
                 (imaginaries, real_beam * imaginary + imaginary_beam * real),
@@ -306,18 +330,18 @@
                 found.append(sum(value[k:k + 8] for k in range(0, rank, 8)))
         return folded(reals + imaginaries)
 
-    def group_beam(f, g, field):
-        return group_back(f, g, group_project(f, g, field))
+    def group_beam(source, g, field):
+        return group_back(source, g, group_project(source, g, field))
 
     def project(f, ref):
         if f in matrix:
             return matrix_project(f, ref[f])
-        return [group_project(f, g, ref[f, group(g)]) for g in range(groups)]
+        return [group_project(owned(f), g, ref[f, group(g)]) for g in range(groups)]
 
     def back(f, seen):
         if f in matrix:
             return matrix_back(f, seen)
-        return jnp.concatenate([group_back(f, g, seen[g]) for g in range(groups)], axis=0)
+        return jnp.concatenate([group_back(owned(f), g, seen[g]) for g in range(groups)], axis=0)
 
     def apply_beam(fs, ref):
         fs = [f for f in fs if f in matrix] + [f for f in fs if f in vector]
@@ -344,12 +368,22 @@
     for i, f in enumerate(edges):
         for g in range(groups):
             rows = group(g)
-            image = group_beam(f, g, x_s[f, rows])
+            image = group_beam(owned(f), g, x_s[f, rows])
             y_s[i, rows] = rows_of(rhs_s, at(f))[rows] - image - local_prior(f, x_s, rows)
     for g in range(groups):
         send(1, g)
-
-    for f in inner:
+    first, rest = [], inner
+    if paired:
+        even_only([lend(k) for k in range(3)])
+        first, rest = inner[:1], inner[1:]
+
+    for f in first:
+        beam_copies[f].wait()
+        r_s[f] = rows_of(rhs_s, at(f)) - back(f, project(f, x_s)) - local_prior(f, x_s)
+    if paired:
+        even_only([lend(3)])
+
+    for f in rest:
         beam_copies[f].wait()
     for i, f in enumerate(matrix):
         for a in range(2):
@@ -357,7 +391,7 @@
             high, low = split(beam_s[f, :, a].reshape(width, ell))
             high_s[i, rows] = high
             low_s[i, rows] = low
-    for f, image in apply_beam(inner, x_s).items():
+    for f, image in apply_beam(rest, x_s).items():
         r_s[f] = rows_of(rhs_s, at(f)) - image - local_prior(f, x_s)
     for f, image in apply_beam(inner, r_s).items():
         u_s[f] = image + local_prior(f, r_s) if f in apart else image
@@ -371,14 +405,21 @@
             halo = jnp.concatenate([first_s[i, 4 * g:4 * g + 4, b, :] for b in range(2)], axis=0)
             r_s[f, rows] = y_s[i, rows] + smooth * halo
         for i, f in enumerate(edges):
-            v_s[i, rows] = group_beam(f, g, r_s[f, rows]) + local_prior(f, r_s, rows)
-        if paired:
-            pl.when(jnp.logical_not(helper))(lambda: cross_copy(g).start())
-        else:
-            send(2, g)
-    if paired:
-        for g in range(groups):
-            send(2, g)
+            v_s[i, rows] = group_beam(owned(f), g, r_s[f, rows]) + local_prior(f, r_s, rows)
+        send(2, g)
+    if paired:
+        @pl.when(helper)
+        def _():
+            for k in range(4):
+                lend(k).wait_recv()
+            for g in range(groups):
+                first_copy(g).wait_recv()
+                rows = group(g)
+                halo = jnp.concatenate([lent_first_s[4 * g:4 * g + 4, b, :] for b in range(2)], axis=0)
+                r = lent_y_s[rows] + smooth * halo
+                local = power * r + smooth * (count(0) * r - lent_r_s[rows])
+                lent_v_s[rows] = group_beam(lent, g, r) + local
+                cross_copy(g).start()
 
     for f in beside_edge:
         u_s[f] = u_s[f] + local_prior(f, r_s)
@@ -390,7 +431,7 @@
         u_s[f] = v_s[i] - beside(i, smooth * (halo_s[0, i] + smooth * x_s[f]))
     if paired:
         pull_s[...] = smooth * u_s[0]
-        pl.when(jnp.logical_not(helper))(lambda: pull_copy().start())
+        even_only([pull_copy()])
     seen |= {f: project(f, u_s) for f in edges}
     norm = jnp.zeros((2 * modes, ell), F32)
     curve, square, cube = norm, norm, norm
@@ -472,14 +513,18 @@
             late_s[my_ma // 2] = message
             message_s[1] = message
             share_all(1, late_s, my_ma // 2, 1, nf)
+            for g in range(groups):
+                cross_copy(g).wait_send()
 
         @pl.when(jnp.logical_not(helper))
         def _():
             for g in range(groups):
                 arrive(2, g)
             pull_copy().wait_send()
+            for k in range(4):
+                lend(k).wait_send()
             for g in range(groups):
-                cross_copy(g).wait_send()
+                first_copy(g).wait_send()
 
         w_s[0] = w_s[0] - smooth * (halo_s[1, 0] - smooth * r_s[0])
     else:
@@ -550,7 +595,7 @@
     dma = pltpu.SemaphoreType.DMA
     pl.run_scoped(
         functools.partial(kernel, nma, nf, *refs),
-        dma((7,)), dma((freqs,)), dma((3, modes // 4, sides)), dma((2,)),
+        dma((7,)), dma((freqs,)), dma((3, modes // 4, sides)), dma((2 * (modes // 4) + 5,)), dma((2,)),
     )
 
 
@@ -576,6 +621,7 @@
     field = pltpu.VMEM(right_side.shape, F32)
     edge = pltpu.VMEM((sides, modes, 2, ell), F32)
     slab = pltpu.VMEM((freqs, 2 * modes, ell), F32)
+    edge_field = pltpu.VMEM((2 * modes, ell), F32)
     edge_slab = pltpu.VMEM((sides, 2 * modes, ell), F32)
     vector = max(min(nf - 1, 2), freqs // 2)
     matrix = max(freqs - vector, 1)
@@ -597,13 +643,14 @@
             edge,
             pltpu.VMEM((2, sides, 2 * modes, ell), F32),
             field, field,
-            pltpu.VMEM((2 * modes, ell), F32), pltpu.VMEM((2 * modes, ell), F32),
-            pltpu.VMEM((2 * modes, ell), F32),
+            edge_field, edge_field, edge_field,
+            pltpu.VMEM((modes, 2, rank, ell), F32), pltpu.VMEM((modes, rank, 128), F32),
+            edge_field, edge_field, pltpu.VMEM((modes, 2, ell), F32), edge_field,
             pltpu.VMEM((2, 1, 128), F32),
             pltpu.VMEM((nma * nf, 1, 128), F32),
-            pltpu.VMEM((nma // 2 if nf == 2 and nma % 2 == 0 else nma * nf, 1, 128), F32),
+            pltpu.VMEM((nma // 2 if nf == 2 and nma % 2 == 0 and freqs > 1 else nma * nf, 1, 128), F32),
             pltpu.SemaphoreType.DMA((3, modes // 4, sides)),
-            pltpu.SemaphoreType.DMA((2 * (modes // 4) + 2,)),
+            pltpu.SemaphoreType.DMA((2 * (modes // 4) + 5,)),
             pltpu.SemaphoreType.DMA((2,)),
             pltpu.SemaphoreType.REGULAR((max((nma * nf).bit_length() - 4, 1),)),
         ],

time: 16.3 us -> 16 us (0.982)
  Pallas kernels: 15.5 us -> 15.2 us
    pallas_call x1, Pallas kernels: 14.8 us -> 14.5 us  [shards(): pl.pallas_call(functools.partial(scoped_kernel, nma, nf, sides), out_shap...]
where the time goes in v6:
time: 16 us; the launch traced here: 15.8 us
  Pallas kernels  15.2 us (95%)
  between operations  0.64 us (4%)
    pallas_call x1, Pallas kernels, shards(): pl.pallas_call(functools.partial(scoped_kernel, nma, nf, sides), out_shap...  14.5 us
    pallas_call x1, Pallas kernels, shards(): pl.pallas_call(write_out, out_shape=[jax.ShapeDtypeStruct(right_side.shap...  0.72 us

profile of v6, /device:TPU:0, one launch (start us, length us, event | category | flops | bytes accessed | tf_op | source)
XLA Modules:
  0.0 15.8 jit_solution(802898422302138000)
XLA Ops:
  0.6 14.5 %solve.1 = (f32[8,4,2,512]{3,2,1,0:T(2,128)S(1)}, f32[8,4,2,512]{3,2,1,0:T(2,128)S(1)}) custom-call(f32[8,4,2,512]{3,2,1,0:T(2,128)} %refs_0_.1, f32[8,4,2,512]{3,2,1,0:T(2,128)} %refs_1_.1, f32[8,4,2,16,512]{4,3,2,1,0:T(8,128)} %refs_2_.1, f32[8,4,16]{2,1,0:T(4,128)} %refs_3_.1, f32[1,512]{1,0:T(1,128)} %bitcast.2, f32[1,512]{1,0:T(1,128)} %bitcast.3), custom_call_target="tpu_custom_call" | custom-call | tf_op jit(solution)/shard_map/solve/pallas_call | solution.py:629
  15.1 0.7 %write_out.1 = (f32[8,4,2,512]{3,2,1,0:T(2,128)}, f32[8,4,2,512]{3,2,1,0:T(2,128)}) custom-call(f32[8,4,2,512]{3,2,1,0:T(2,128)S(1)} %get-tuple-element.4.sol_in, f32[8,4,2,512]{3,2,1,0:T(2,128)S(1)} %get-tuple-element.5.res_in), custom_call_target="tpu_custom_call" | custom-call | tf_op jit(solution)/shard_map/write_out/pallas_call | solution.py:662

commit v7 on v6

--- a/solution.py
+++ b/solution.py
@@ -128,8 +128,7 @@
     for i, device in enumerate(greeted):
         greet(device)
         if i == 0:
-            others = [beam_copies[f] for f in edges] + [rhs_copy] + [beam_copies[f] for f in inner]
-            for copy in [x0_copy] + small + others:
+            for copy in [beam_copies[f] for f in edges] + [x0_copy, rhs_copy] + small:
                 copy.start()
     expected = len(greeted)
     if nf > 2:
@@ -235,11 +234,14 @@
 
     for copy in edge_copies:
         copy.wait()
+    for f in inner:
+        beam_copies[f].start()
     pl.semaphore_wait(barrier, expected)
-    for g in range(groups):
-        send(0, g)
-    if paired:
-        even_only([first_copy(g) for g in range(groups)])
+    if paired:
+        even_only([near_copy(0, g) for g in range(groups)] + [first_copy(g) for g in range(groups)])
+    else:
+        for g in range(groups):
+            send(0, g)
     advance()
 
     x0_copy.wait()
@@ -370,6 +372,12 @@
             rows = group(g)
             image = group_beam(owned(f), g, x_s[f, rows])
             y_s[i, rows] = rows_of(rhs_s, at(f))[rows] - image - local_prior(f, x_s, rows)
+    if paired:
+        @pl.when(helper)
+        def _():
+            for g in range(groups):
+                near_copy(0, g).start()
+
     for g in range(groups):
         send(1, g)
     first, rest = [], inner
@@ -398,6 +406,20 @@
     seen = {f: project(f, u_s) for f in apart}
     advance()
 
+    if paired:
+        @pl.when(helper)
+        def _():
+            for k in range(4):
+                lend(k).wait_recv()
+            for g in range(groups):
+                first_copy(g).wait_recv()
+                rows = group(g)
+                halo = jnp.concatenate([lent_first_s[4 * g:4 * g + 4, b, :] for b in range(2)], axis=0)
+                r = lent_y_s[rows] + smooth * halo
+                local = power * r + smooth * (count(0) * r - lent_r_s[rows])
+                lent_v_s[rows] = group_beam(lent, g, r) + local
+                cross_copy(g).start()
+
     for g in range(groups):
         arrive(0, g)
         rows = group(g)
@@ -407,20 +429,6 @@
         for i, f in enumerate(edges):
             v_s[i, rows] = group_beam(owned(f), g, r_s[f, rows]) + local_prior(f, r_s, rows)
         send(2, g)
-    if paired:
-        @pl.when(helper)
-        def _():
-            for k in range(4):
-                lend(k).wait_recv()
-            for g in range(groups):
-                first_copy(g).wait_recv()
-                rows = group(g)
-                halo = jnp.concatenate([lent_first_s[4 * g:4 * g + 4, b, :] for b in range(2)], axis=0)
-                r = lent_y_s[rows] + smooth * halo
-                local = power * r + smooth * (count(0) * r - lent_r_s[rows])
-                lent_v_s[rows] = group_beam(lent, g, r) + local
-                cross_copy(g).start()
-
     for f in beside_edge:
         u_s[f] = u_s[f] + local_prior(f, r_s)
     seen |= {f: project(f, u_s) for f in beside_edge}

time: 16 us -> 17 us (1.062)
  Pallas kernels: 15.2 us -> 16.2 us
    pallas_call x1, Pallas kernels: 14.5 us -> 15.5 us  [shards(): pl.pallas_call(functools.partial(scoped_kernel, nma, nf, sides), out_shap...]
where the time goes in v7:
time: 17 us; the launch traced here: 16.8 us
  Pallas kernels  16.2 us (95%)
  between operations  0.64 us (4%)
    pallas_call x1, Pallas kernels, shards(): pl.pallas_call(functools.partial(scoped_kernel, nma, nf, sides), out_shap...  15.5 us
    pallas_call x1, Pallas kernels, shards(): pl.pallas_call(write_out, out_shape=[jax.ShapeDtypeStruct(right_side.shap...  0.72 us

profile of v7, /device:TPU:0, one launch (start us, length us, event | category | flops | bytes accessed | tf_op | source)
XLA Modules:
  0.0 16.8 jit_solution(3482706982608271734)
XLA Ops:
  0.6 15.5 %solve.1 = (f32[8,4,2,512]{3,2,1,0:T(2,128)S(1)}, f32[8,4,2,512]{3,2,1,0:T(2,128)S(1)}) custom-call(f32[8,4,2,512]{3,2,1,0:T(2,128)} %refs_0_.1, f32[8,4,2,512]{3,2,1,0:T(2,128)} %refs_1_.1, f32[8,4,2,16,512]{4,3,2,1,0:T(8,128)} %refs_2_.1, f32[8,4,16]{2,1,0:T(4,128)} %refs_3_.1, f32[1,512]{1,0:T(1,128)} %bitcast.2, f32[1,512]{1,0:T(1,128)} %bitcast.3), custom_call_target="tpu_custom_call" | custom-call | tf_op jit(solution)/shard_map/solve/pallas_call | solution.py:637
  16.1 0.7 %write_out.1 = (f32[8,4,2,512]{3,2,1,0:T(2,128)}, f32[8,4,2,512]{3,2,1,0:T(2,128)}) custom-call(f32[8,4,2,512]{3,2,1,0:T(2,128)S(1)} %get-tuple-element.4.sol_in, f32[8,4,2,512]{3,2,1,0:T(2,128)S(1)} %get-tuple-element.5.res_in), custom_call_target="tpu_custom_call" | custom-call | tf_op jit(solution)/shard_map/write_out/pallas_call | solution.py:670

commit v8 on v7

--- a/solution.py
+++ b/solution.py
@@ -238,7 +238,7 @@
         beam_copies[f].start()
     pl.semaphore_wait(barrier, expected)
     if paired:
-        even_only([near_copy(0, g) for g in range(groups)] + [first_copy(g) for g in range(groups)])
+        even_only([first_copy(g) for g in range(groups)] + [near_copy(0, g) for g in range(groups)])
     else:
         for g in range(groups):
             send(0, g)
@@ -372,24 +372,25 @@
             rows = group(g)
             image = group_beam(owned(f), g, x_s[f, rows])
             y_s[i, rows] = rows_of(rhs_s, at(f))[rows] - image - local_prior(f, x_s, rows)
-    if paired:
-        @pl.when(helper)
-        def _():
-            for g in range(groups):
-                near_copy(0, g).start()
-
-    for g in range(groups):
-        send(1, g)
     first, rest = [], inner
     if paired:
-        even_only([lend(k) for k in range(3)])
+        even_only([near_copy(1, g) for g in range(groups)] + [lend(k) for k in range(3)])
         first, rest = inner[:1], inner[1:]
+    else:
+        for g in range(groups):
+            send(1, g)
 
     for f in first:
         beam_copies[f].wait()
         r_s[f] = rows_of(rhs_s, at(f)) - back(f, project(f, x_s)) - local_prior(f, x_s)
     if paired:
         even_only([lend(3)])
+
+        @pl.when(helper)
+        def _():
+            for kind in range(2):
+                for g in range(groups):
+                    near_copy(kind, g).start()
 
     for f in rest:
         beam_copies[f].wait()
@@ -428,7 +429,10 @@
             r_s[f, rows] = y_s[i, rows] + smooth * halo
         for i, f in enumerate(edges):
             v_s[i, rows] = group_beam(owned(f), g, r_s[f, rows]) + local_prior(f, r_s, rows)
-        send(2, g)
+        if paired:
+            pl.when(helper)(lambda: near_copy(2, g).start())
+        else:
+            send(2, g)
     for f in beside_edge:
         u_s[f] = u_s[f] + local_prior(f, r_s)
     seen |= {f: project(f, u_s) for f in beside_edge}
@@ -502,6 +506,8 @@
         return sum(x[:, i:i + 128] for i in range(0, ell, 128))
 
     share_all(0, early_s, me, 0, 1)
+    if paired:
+        even_only([near_copy(2, g) for g in range(groups)])
     for f in matrix + vector:
         w_s[f] = w_s[f] + back(f, seen[f])
 

time: 17 us -> 16.2 us (0.953)
  Pallas kernels: 16.2 us -> 15.5 us
    pallas_call x1, Pallas kernels: 15.5 us -> 14.7 us  [shards(): pl.pallas_call(functools.partial(scoped_kernel, nma, nf, sides), out_shap...]
where the time goes in v8:
time: 16.2 us; the launch traced here: 16.1 us
  Pallas kernels  15.5 us (96%)
  between operations  0.64 us (4%)
    pallas_call x1, Pallas kernels, shards(): pl.pallas_call(functools.partial(scoped_kernel, nma, nf, sides), out_shap...  14.7 us
    pallas_call x1, Pallas kernels, shards(): pl.pallas_call(write_out, out_shape=[jax.ShapeDtypeStruct(right_side.shap...  0.72 us

profile of v8, /device:TPU:0, one launch (start us, length us, event | category | flops | bytes accessed | tf_op | source)
XLA Modules:
  0.0 16.1 jit_solution(4302280706710947487)
XLA Ops:
  0.6 14.7 %solve.1 = (f32[8,4,2,512]{3,2,1,0:T(2,128)S(1)}, f32[8,4,2,512]{3,2,1,0:T(2,128)S(1)}) custom-call(f32[8,4,2,512]{3,2,1,0:T(2,128)} %refs_0_.1, f32[8,4,2,512]{3,2,1,0:T(2,128)} %refs_1_.1, f32[8,4,2,16,512]{4,3,2,1,0:T(8,128)} %refs_2_.1, f32[8,4,16]{2,1,0:T(4,128)} %refs_3_.1, f32[1,512]{1,0:T(1,128)} %bitcast.2, f32[1,512]{1,0:T(1,128)} %bitcast.3), custom_call_target="tpu_custom_call" | custom-call | tf_op jit(solution)/shard_map/solve/pallas_call | solution.py:643
  15.4 0.7 %write_out.1 = (f32[8,4,2,512]{3,2,1,0:T(2,128)}, f32[8,4,2,512]{3,2,1,0:T(2,128)}) custom-call(f32[8,4,2,512]{3,2,1,0:T(2,128)S(1)} %get-tuple-element.4.sol_in, f32[8,4,2,512]{3,2,1,0:T(2,128)S(1)} %get-tuple-element.5.res_in), custom_call_target="tpu_custom_call" | custom-call | tf_op jit(solution)/shard_map/write_out/pallas_call | solution.py:676

commit v9 on v6

--- a/solution.py
+++ b/solution.py
@@ -54,7 +54,7 @@
     nma, nf, rhs_in, x0_in, beam_in, noise_in, power_in, smooth_in, sol_s, res_s,
     rhs_s, x0_s, edge_s, beam_s, noise_s, power_s, smooth_s,
     high_s, low_s, x_s, y_s, r_s, v_s, u_s, w_s, mask_s, column_s, first_s, halo_s,
-    sol_move_s, res_move_s, pull_s, partner_s, cross_s,
+    r_out_s, u_out_s, w_out_s, pull_s, partner_s, cross_s,
     lent_beam_s, lent_column_s, lent_y_s, lent_r_s, lent_first_s, lent_v_s,
     message_s, early_s, late_s,
     halo_recv, pair_recv, sum_recv, word_sem, in_sem, beam_sem, halo_send, pair_send, sum_send,
@@ -128,8 +128,7 @@
     for i, device in enumerate(greeted):
         greet(device)
         if i == 0:
-            others = [beam_copies[f] for f in edges] + [rhs_copy] + [beam_copies[f] for f in inner]
-            for copy in [x0_copy] + small + others:
+            for copy in [beam_copies[f] for f in edges] + [x0_copy, rhs_copy] + small:
                 copy.start()
     expected = len(greeted)
     if nf > 2:
@@ -235,6 +234,8 @@
 
     for copy in edge_copies:
         copy.wait()
+    for f in inner:
+        beam_copies[f].start()
     pl.semaphore_wait(barrier, expected)
     for g in range(groups):
         send(0, g)
@@ -370,18 +371,24 @@
             rows = group(g)
             image = group_beam(owned(f), g, x_s[f, rows])
             y_s[i, rows] = rows_of(rhs_s, at(f))[rows] - image - local_prior(f, x_s, rows)
-    for g in range(groups):
-        send(1, g)
     first, rest = [], inner
     if paired:
-        even_only([lend(k) for k in range(3)])
+        even_only([near_copy(1, g) for g in range(groups)] + [lend(k) for k in range(3)])
         first, rest = inner[:1], inner[1:]
+    else:
+        for g in range(groups):
+            send(1, g)
 
     for f in first:
         beam_copies[f].wait()
         r_s[f] = rows_of(rhs_s, at(f)) - back(f, project(f, x_s)) - local_prior(f, x_s)
     if paired:
         even_only([lend(3)])
+
+        @pl.when(helper)
+        def _():
+            for g in range(groups):
+                near_copy(1, g).start()
 
     for f in rest:
         beam_copies[f].wait()
@@ -406,7 +413,10 @@
             r_s[f, rows] = y_s[i, rows] + smooth * halo
         for i, f in enumerate(edges):
             v_s[i, rows] = group_beam(owned(f), g, r_s[f, rows]) + local_prior(f, r_s, rows)
-        send(2, g)
+        if paired:
+            pl.when(helper)(lambda: near_copy(2, g).start())
+        else:
+            send(2, g)
     if paired:
         @pl.when(helper)
         def _():
@@ -494,6 +504,8 @@
         return sum(x[:, i:i + 128] for i in range(0, ell, 128))
 
     share_all(0, early_s, me, 0, 1)
+    if paired:
+        even_only([near_copy(2, g) for g in range(groups)])
     for f in matrix + vector:
         w_s[f] = w_s[f] + back(f, seen[f])
 
@@ -547,47 +559,45 @@
     for kind in range(3):
         for g in range(groups):
             sent(kind, g)
+    for source, target in ((r_s, r_out_s), (u_s, u_out_s), (w_s, w_out_s)):
+        for f in range(freqs):
+            value = source[f]
+            for g in range(groups):
+                for b in range(2):
+                    start = 8 * g + 4 * b
+                    target[4 * g:4 * g + 4, at(f), b, :] = value[start:start + 4]
+
+    landed(early_s, sum_send.at[0], n - 1)
     landed(early_s, sum_recv.at[0], n - 1)
+    if paired:
+        @pl.when(helper)
+        def _():
+            rows = early_s.at[pl.ds(0, nma - 1)]
+            pltpu.make_async_copy(rows, rows, sum_send.at[1]).wait()
+            landed(late_s, sum_recv.at[1], late_rows - 1)
+
+        pl.when(jnp.logical_not(helper))(lambda: landed(late_s, sum_recv.at[1], late_rows))
+    else:
+        landed(late_s, sum_send.at[1], late_rows - 1)
+        landed(late_s, sum_recv.at[1], late_rows - 1)
     total = jnp.sum(early_s[...], axis=0)
     m0, m1, m2, m3, known = (
         jnp.sum(jnp.where(lane == i, total, 0.0), axis=1, keepdims=True)
         for i in (0, 1, 2, 3, 4 + my_f)
     )
-    if paired:
-        m3 = m3 + 2.0 * known
-    step = m0 / m1
-    norm_next = step * (step * m2 - m1)
-    growth = norm_next / m0
-    curve_part = m1 - 2.0 * step * m2 + step * step * m3 - growth * norm_next / step
-    cross_scale = step * step * (2.0 if paired else 1.0)
-    for f in range(freqs):
-        x, r, u, w = x_s[f], r_s[f], u_s[f], w_s[f]
-        for target, value in (
-            (sol_s, x + step * r),
-            (res_s, r - step * u),
-            (sol_move_s, (1.0 + growth) * r - step * u),
-            (res_move_s, (1.0 + growth) * u - step * w),
-        ):
-            for g in range(groups):
-                for b in range(2):
-                    start = 8 * g + 4 * b
-                    target[4 * g:4 * g + 4, at(f), b, :] = value[start:start + 4]
-    landed(early_s, sum_send.at[0], n - 1)
-    if paired:
-        @pl.when(helper)
-        def _():
-            rows = early_s.at[pl.ds(0, nma - 1)]
-            pltpu.make_async_copy(rows, rows, sum_send.at[1]).wait()
-            landed(late_s, sum_recv.at[1], late_rows - 1)
-
-        pl.when(jnp.logical_not(helper))(lambda: landed(late_s, sum_recv.at[1], late_rows))
-    else:
-        landed(late_s, sum_send.at[1], late_rows - 1)
-        landed(late_s, sum_recv.at[1], late_rows - 1)
     crossed = jnp.sum(jnp.sum(late_s[...], axis=0), axis=1, keepdims=True)
-    step_next = norm_next / (curve_part - cross_scale * crossed)
-    sol_s[...] = sol_s[...] + step_next * sol_move_s[...]
-    res_s[...] = res_s[...] - step_next * res_move_s[...]
+    m3 = m3 - 2.0 * (crossed - known) if paired else m3 - crossed
+    inverse = 1.0 / m1
+    step = m0 * inverse
+    drop = step * m2 - m1
+    growth = drop * inverse
+    curve_next = m1 - 2.0 * step * m2 + step * step * m3
+    step_next = step * drop / (curve_next - growth * drop)
+    c = step + step_next * (1.0 + growth)
+    e = step * step_next
+    r, u = r_out_s[...], u_out_s[...]
+    sol_s[...] = x0_s[...] + c * r - e * u
+    res_s[...] = r - c * u + e * w_out_s[...]
 
 
 def scoped_kernel(nma, nf, sides, *refs):
@@ -642,7 +652,7 @@
             pltpu.VMEM((vector, modes, rank, 128), F32),
             edge,
             pltpu.VMEM((2, sides, 2 * modes, ell), F32),
-            field, field,
+            field, field, field,
             edge_field, edge_field, edge_field,
             pltpu.VMEM((modes, 2, rank, ell), F32), pltpu.VMEM((modes, rank, 128), F32),
             edge_field, edge_field, pltpu.VMEM((modes, 2, ell), F32), edge_field,

time: 16 us -> 16.2 us (1.012)
  Pallas kernels: 15.2 us -> 15.4 us
    pallas_call x1, Pallas kernels: 14.5 us -> 14.7 us  [shards(): pl.pallas_call(functools.partial(scoped_kernel, nma, nf, sides), out_shap...]
where the time goes in v9:
time: 16.2 us; the launch traced here: 16.1 us
  Pallas kernels  15.4 us (95%)
  between operations  0.64 us (4%)
    pallas_call x1, Pallas kernels, shards(): pl.pallas_call(functools.partial(scoped_kernel, nma, nf, sides), out_shap...  14.7 us
    pallas_call x1, Pallas kernels, shards(): pl.pallas_call(write_out, out_shape=[jax.ShapeDtypeStruct(right_side.shap...  0.72 us

profile of v9, /device:TPU:0, one launch (start us, length us, event | category | flops | bytes accessed | tf_op | source)
XLA Modules:
  0.0 16.1 jit_solution(14396935223029783406)
XLA Ops:
  0.6 14.7 %solve.1 = (f32[8,4,2,512]{3,2,1,0:T(2,128)S(1)}, f32[8,4,2,512]{3,2,1,0:T(2,128)S(1)}) custom-call(f32[8,4,2,512]{3,2,1,0:T(2,128)} %refs_0_.1, f32[8,4,2,512]{3,2,1,0:T(2,128)} %refs_1_.1, f32[8,4,2,16,512]{4,3,2,1,0:T(8,128)} %refs_2_.1, f32[8,4,16]{2,1,0:T(4,128)} %refs_3_.1, f32[1,512]{1,0:T(1,128)} %bitcast.2, f32[1,512]{1,0:T(1,128)} %bitcast.3), custom_call_target="tpu_custom_call" | custom-call | tf_op jit(solution)/shard_map/solve/pallas_call | solution.py:639
  15.3 0.7 %write_out.1 = (f32[8,4,2,512]{3,2,1,0:T(2,128)}, f32[8,4,2,512]{3,2,1,0:T(2,128)}) custom-call(f32[8,4,2,512]{3,2,1,0:T(2,128)S(1)} %get-tuple-element.4.sol_in, f32[8,4,2,512]{3,2,1,0:T(2,128)S(1)} %get-tuple-element.5.res_in), custom_call_target="tpu_custom_call" | custom-call | tf_op jit(solution)/shard_map/write_out/pallas_call | solution.py:672

commit v10 on v9

--- a/solution.py
+++ b/solution.py
@@ -57,7 +57,7 @@
     r_out_s, u_out_s, w_out_s, pull_s, partner_s, cross_s,
     lent_beam_s, lent_column_s, lent_y_s, lent_r_s, lent_first_s, lent_v_s,
     message_s, early_s, late_s,
-    halo_recv, pair_recv, sum_recv, word_sem, in_sem, beam_sem, halo_send, pair_send, sum_send,
+    halo_recv, pair_recv, sum_recv, word_sem, in_sem, beam_sem, halo_send, pair_send, hand_send, sum_send,
 ):
     modes, freqs, _, ell = rhs_in.shape
     rank = beam_in.shape[3]
@@ -217,6 +217,14 @@
         rows = pl.ds(8 * g, 8)
         return pair_copy(5 + groups + g, lent_v_s.at[rows], cross_s.at[rows], my_ma, 1 - my_f)
 
+    def hand_copy(g):
+        rows = pl.ds(4 * g, 4)
+        return pltpu.make_async_remote_copy(
+            src_ref=lent_first_s.at[rows], dst_ref=first_s.at[0, rows],
+            send_sem=hand_send.at[g], recv_sem=halo_recv.at[0, g, 0],
+            device_id=(my_ma - 1, my_f), device_id_type=MESH,
+        )
+
     def even_only(copies):
         @pl.when(jnp.logical_not(helper))
         def _():
@@ -237,10 +245,16 @@
     for f in inner:
         beam_copies[f].start()
     pl.semaphore_wait(barrier, expected)
-    for g in range(groups):
-        send(0, g)
     if paired:
         even_only([first_copy(g) for g in range(groups)])
+
+        @pl.when(helper)
+        def _():
+            for g in range(groups):
+                near_copy(0, g).start()
+    else:
+        for g in range(groups):
+            send(0, g)
     advance()
 
     x0_copy.wait()
@@ -420,10 +434,12 @@
     if paired:
         @pl.when(helper)
         def _():
+            for g in range(groups):
+                first_copy(g).wait_recv()
+                hand_copy(g).start()
             for k in range(4):
                 lend(k).wait_recv()
             for g in range(groups):
-                first_copy(g).wait_recv()
                 rows = group(g)
                 halo = jnp.concatenate([lent_first_s[4 * g:4 * g + 4, b, :] for b in range(2)], axis=0)
                 r = lent_y_s[rows] + smooth * halo
@@ -556,9 +572,20 @@
         for f, rows, pull in nexts:
             w_s[f, rows] = w_s[f, rows] - pull
 
-    for kind in range(3):
+    if paired:
         for g in range(groups):
-            sent(kind, g)
+            for kind in (1, 2):
+                sent(kind, g)
+
+        @pl.when(helper)
+        def _():
+            for g in range(groups):
+                sent(0, g)
+                hand_copy(g).wait_send()
+    else:
+        for kind in range(3):
+            for g in range(groups):
+                sent(kind, g)
     for source, target in ((r_s, r_out_s), (u_s, u_out_s), (w_s, w_out_s)):
         for f in range(freqs):
             value = source[f]
@@ -605,7 +632,8 @@
     dma = pltpu.SemaphoreType.DMA
     pl.run_scoped(
         functools.partial(kernel, nma, nf, *refs),
-        dma((7,)), dma((freqs,)), dma((3, modes // 4, sides)), dma((2 * (modes // 4) + 5,)), dma((2,)),
+        dma((7,)), dma((freqs,)), dma((3, modes // 4, sides)), dma((2 * (modes // 4) + 5,)),
+        dma((modes // 4,)), dma((2,)),
     )
 
 

time: 16.2 us -> 15.9 us (0.981)
  Pallas kernels: 15.4 us -> 15.1 us
    pallas_call x1, Pallas kernels: 14.7 us -> 14.4 us  [shards(): pl.pallas_call(functools.partial(scoped_kernel, nma, nf, sides), out_shap...]
where the time goes in v10:
time: 15.9 us; the launch traced here: 15.7 us
  Pallas kernels  15.1 us (95%)
  between operations  0.64 us (4%)
    pallas_call x1, Pallas kernels, shards(): pl.pallas_call(functools.partial(scoped_kernel, nma, nf, sides), out_shap...  14.4 us
    pallas_call x1, Pallas kernels, shards(): pl.pallas_call(write_out, out_shape=[jax.ShapeDtypeStruct(right_side.shap...  0.72 us

profile of v10, /device:TPU:0, one launch (start us, length us, event | category | flops | bytes accessed | tf_op | source)
XLA Modules:
  0.0 15.7 jit_solution(9155003086254479062)
XLA Ops:
  0.6 14.4 %solve.1 = (f32[8,4,2,512]{3,2,1,0:T(2,128)S(1)}, f32[8,4,2,512]{3,2,1,0:T(2,128)S(1)}) custom-call(f32[8,4,2,512]{3,2,1,0:T(2,128)} %refs_0_.1, f32[8,4,2,512]{3,2,1,0:T(2,128)} %refs_1_.1, f32[8,4,2,16,512]{4,3,2,1,0:T(8,128)} %refs_2_.1, f32[8,4,16]{2,1,0:T(4,128)} %refs_3_.1, f32[1,512]{1,0:T(1,128)} %bitcast.2, f32[1,512]{1,0:T(1,128)} %bitcast.3), custom_call_target="tpu_custom_call" | custom-call | tf_op jit(solution)/shard_map/solve/pallas_call | solution.py:667
  15.0 0.7 %write_out.1 = (f32[8,4,2,512]{3,2,1,0:T(2,128)}, f32[8,4,2,512]{3,2,1,0:T(2,128)}) custom-call(f32[8,4,2,512]{3,2,1,0:T(2,128)S(1)} %get-tuple-element.4.sol_in, f32[8,4,2,512]{3,2,1,0:T(2,128)S(1)} %get-tuple-element.5.res_in), custom_call_target="tpu_custom_call" | custom-call | tf_op jit(solution)/shard_map/write_out/pallas_call | solution.py:700

commit v11 on v10

--- a/solution.py
+++ b/solution.py
@@ -55,7 +55,7 @@
     rhs_s, x0_s, edge_s, beam_s, noise_s, power_s, smooth_s,
     high_s, low_s, x_s, y_s, r_s, v_s, u_s, w_s, mask_s, column_s, first_s, halo_s,
     r_out_s, u_out_s, w_out_s, pull_s, partner_s, cross_s,
-    lent_beam_s, lent_column_s, lent_y_s, lent_r_s, lent_first_s, lent_v_s,
+    lent_beam_s, lent_column_s, lent_y_s, lent_r_s, lent_first_s, lent_v_s, ahead_s,
     message_s, early_s, late_s,
     halo_recv, pair_recv, sum_recv, word_sem, in_sem, beam_sem, halo_send, pair_send, hand_send, sum_send,
 ):
@@ -217,6 +217,14 @@
         rows = pl.ds(8 * g, 8)
         return pair_copy(5 + groups + g, lent_v_s.at[rows], cross_s.at[rows], my_ma, 1 - my_f)
 
+    def ahead_copy(g):
+        rows = pl.ds(8 * g, 8)
+        return pltpu.make_async_remote_copy(
+            src_ref=ahead_s.at[rows], dst_ref=halo_s.at[1, 0, rows],
+            send_sem=halo_send.at[2, g, 0], recv_sem=halo_recv.at[2, g, 0],
+            device_id=(my_ma, 1 - my_f), device_id_type=MESH,
+        )
+
     def hand_copy(g):
         rows = pl.ds(4 * g, 4)
         return pltpu.make_async_remote_copy(
@@ -416,30 +424,31 @@
         r_s[f] = rows_of(rhs_s, at(f)) - image - local_prior(f, x_s)
     for f, image in apply_beam(inner, r_s).items():
         u_s[f] = image + local_prior(f, r_s) if f in apart else image
-    seen = {f: project(f, u_s) for f in apart}
     advance()
 
-    for g in range(groups):
-        arrive(0, g)
+    def complete(i, f, g):
         rows = group(g)
-        for i, f in enumerate(edges):
-            halo = jnp.concatenate([first_s[i, 4 * g:4 * g + 4, b, :] for b in range(2)], axis=0)
-            r_s[f, rows] = y_s[i, rows] + smooth * halo
-        for i, f in enumerate(edges):
-            v_s[i, rows] = group_beam(owned(f), g, r_s[f, rows]) + local_prior(f, r_s, rows)
-        if paired:
-            pl.when(helper)(lambda: near_copy(2, g).start())
-        else:
-            send(2, g)
+        halo = jnp.concatenate([first_s[i, 4 * g:4 * g + 4, b, :] for b in range(2)], axis=0)
+        r_s[f, rows] = y_s[i, rows] + smooth * halo
+
+    def edge_image(f, g):
+        rows = group(g)
+        return group_beam(owned(f), g, r_s[f, rows]) + local_prior(f, r_s, rows)
+
     if paired:
         @pl.when(helper)
         def _():
+            for g in range(groups):
+                arrive(0, g)
+                complete(0, 0, g)
+                ahead_s[group(g)] = edge_image(0, g)
+                ahead_copy(g).start()
             for g in range(groups):
                 first_copy(g).wait_recv()
                 hand_copy(g).start()
-            for k in range(4):
-                lend(k).wait_recv()
-            for g in range(groups):
+                if g == 0:
+                    for k in range(4):
+                        lend(k).wait_recv()
                 rows = group(g)
                 halo = jnp.concatenate([lent_first_s[4 * g:4 * g + 4, b, :] for b in range(2)], axis=0)
                 r = lent_y_s[rows] + smooth * halo
@@ -447,12 +456,31 @@
                 lent_v_s[rows] = group_beam(lent, g, r) + local
                 cross_copy(g).start()
 
+    seen = {f: project(f, u_s) for f in apart}
+    if paired:
+        @pl.when(jnp.logical_not(helper))
+        def _():
+            for g in range(groups):
+                arrive(0, g)
+
+        for g in range(groups):
+            arrive(1, g)
+    for g in range(groups):
+        if not paired:
+            arrive(0, g)
+        for i, f in enumerate(edges):
+            complete(i, f, g)
+        for i, f in enumerate(edges):
+            v_s[i, group(g)] = edge_image(f, g)
+        if not paired:
+            send(2, g)
     for f in beside_edge:
         u_s[f] = u_s[f] + local_prior(f, r_s)
     seen |= {f: project(f, u_s) for f in beside_edge}
 
-    for g in range(groups):
-        arrive(1, g)
+    if not paired:
+        for g in range(groups):
+            arrive(1, g)
     for i, f in enumerate(edges):
         u_s[f] = v_s[i] - beside(i, smooth * (halo_s[0, i] + smooth * x_s[f]))
     if paired:
@@ -683,7 +711,7 @@
             field, field, field,
             edge_field, edge_field, edge_field,
             pltpu.VMEM((modes, 2, rank, ell), F32), pltpu.VMEM((modes, rank, 128), F32),
-            edge_field, edge_field, pltpu.VMEM((modes, 2, ell), F32), edge_field,
+            edge_field, edge_field, pltpu.VMEM((modes, 2, ell), F32), edge_field, edge_field,
             pltpu.VMEM((2, 1, 128), F32),
             pltpu.VMEM((nma * nf, 1, 128), F32),
             pltpu.VMEM((nma // 2 if nf == 2 and nma % 2 == 0 and freqs > 1 else nma * nf, 1, 128), F32),

time: 15.9 us -> 15.7 us (0.987)
  no operation moved by 1% of the time
where the time goes in v11:
time: 15.7 us; the launch traced here: 15.6 us
  Pallas kernels  15 us (96%)
  between operations  0.64 us (4%)
    pallas_call x1, Pallas kernels, shards(): pl.pallas_call(functools.partial(scoped_kernel, nma, nf, sides), out_shap...  14.2 us
    pallas_call x1, Pallas kernels, shards(): pl.pallas_call(write_out, out_shape=[jax.ShapeDtypeStruct(right_side.shap...  0.72 us

profile of v11, /device:TPU:0, one launch (start us, length us, event | category | flops | bytes accessed | tf_op | source)
XLA Modules:
  0.0 15.6 jit_solution(12727220425595020148)
XLA Ops:
  0.6 14.2 %solve.1 = (f32[8,4,2,512]{3,2,1,0:T(2,128)S(1)}, f32[8,4,2,512]{3,2,1,0:T(2,128)S(1)}) custom-call(f32[8,4,2,512]{3,2,1,0:T(2,128)} %refs_0_.1, f32[8,4,2,512]{3,2,1,0:T(2,128)} %refs_1_.1, f32[8,4,2,16,512]{4,3,2,1,0:T(8,128)} %refs_2_.1, f32[8,4,16]{2,1,0:T(4,128)} %refs_3_.1, f32[1,512]{1,0:T(1,128)} %bitcast.2, f32[1,512]{1,0:T(1,128)} %bitcast.3), custom_call_target="tpu_custom_call" | custom-call | tf_op jit(solution)/shard_map/solve/pallas_call | solution.py:695
  14.9 0.7 %write_out.1 = (f32[8,4,2,512]{3,2,1,0:T(2,128)}, f32[8,4,2,512]{3,2,1,0:T(2,128)}) custom-call(f32[8,4,2,512]{3,2,1,0:T(2,128)S(1)} %get-tuple-element.4.sol_in, f32[8,4,2,512]{3,2,1,0:T(2,128)S(1)} %get-tuple-element.5.res_in), custom_call_target="tpu_custom_call" | custom-call | tf_op jit(solution)/shard_map/write_out/pallas_call | solution.py:728

commit v12 on v11

--- a/solution.py
+++ b/solution.py
@@ -457,55 +457,76 @@
                 cross_copy(g).start()
 
     seen = {f: project(f, u_s) for f in apart}
-    if paired:
-        @pl.when(jnp.logical_not(helper))
-        def _():
-            for g in range(groups):
-                arrive(0, g)
-
-        for g in range(groups):
+    grouped = [f for f in beside_edge if f in vector]
+    whole = [f for f in beside_edge if f in matrix]
+    seen |= {f: [] for f in grouped + edges}
+    zero = jnp.zeros((8, ell), F32)
+    sums = [zero, zero, zero, zero]
+    column_part = jnp.zeros((rank, 128), F32)
+
+    def add_up(g, sums, column_part):
+        rows = group(g)
+        norm, curve, square, cube = sums
+        for f in inner + edges:
+            if f in vector:
+                for real, imaginary, real_weighted, imaginary_weighted in seen[f][g]:
+                    column_part = column_part + (real * real_weighted + imaginary * imaginary_weighted)
+            r, u = r_s[f, rows], u_s[f, rows]
+            w = local_prior(f, u_s, rows)
+            w_s[f, rows] = w
+            norm = norm + r * r
+            curve = curve + r * u
+            square = square + u * u
+            cube = cube + u * w
+        return [norm, curve, square, cube], column_part
+
+    def finish_edges(g):
+        rows = group(g)
+        for i, f in enumerate(edges):
+            u_s[f, rows] = v_s[i, rows] - beside(
+                i, smooth * (halo_s[0, i, rows] + smooth * x_s[f, rows])
+            )
+            seen[f].append(group_project(owned(f), g, u_s[f, rows]))
+
+    for g in range(groups):
+        rows = group(g)
+        if paired:
+            pl.when(jnp.logical_not(helper))(lambda: arrive(0, g))
             arrive(1, g)
-    for g in range(groups):
-        if not paired:
+        else:
             arrive(0, g)
         for i, f in enumerate(edges):
             complete(i, f, g)
         for i, f in enumerate(edges):
-            v_s[i, group(g)] = edge_image(f, g)
+            v_s[i, rows] = edge_image(f, g)
         if not paired:
             send(2, g)
-    for f in beside_edge:
+        for f in grouped:
+            u_s[f, rows] = u_s[f, rows] + local_prior(f, r_s, rows)
+            seen[f].append(group_project(owned(f), g, u_s[f, rows]))
+        if paired:
+            finish_edges(g)
+            pull_s[rows] = smooth * u_s[0, rows]
+            if not whole:
+                sums, column_part = add_up(g, sums, column_part)
+    for f in whole:
         u_s[f] = u_s[f] + local_prior(f, r_s)
-    seen |= {f: project(f, u_s) for f in beside_edge}
-
-    if not paired:
+        seen[f] = project(f, u_s)
+    if paired:
+        even_only([pull_copy()])
+    else:
         for g in range(groups):
             arrive(1, g)
-    for i, f in enumerate(edges):
-        u_s[f] = v_s[i] - beside(i, smooth * (halo_s[0, i] + smooth * x_s[f]))
-    if paired:
-        pull_s[...] = smooth * u_s[0]
-        even_only([pull_copy()])
-    seen |= {f: project(f, u_s) for f in edges}
-    norm = jnp.zeros((2 * modes, ell), F32)
-    curve, square, cube = norm, norm, norm
+            finish_edges(g)
+    if whole or not paired:
+        for g in range(groups):
+            sums, column_part = add_up(g, sums, column_part)
     beam_part = jnp.zeros((2 * modes, width), F32)
-    column_part = jnp.zeros((rank, 128), F32)
-    for f in inner + edges:
-        if f in matrix:
-            beam_part = beam_part + seen[f][0] * seen[f][1]
-        else:
-            for parts in seen[f]:
-                for real, imaginary, real_weighted, imaginary_weighted in parts:
-                    column_part = column_part + (real * real_weighted + imaginary * imaginary_weighted)
-        w_s[f] = local_prior(f, u_s)
-        norm = norm + r_s[f] * r_s[f]
-        curve = curve + r_s[f] * u_s[f]
-        square = square + u_s[f] * u_s[f]
-        cube = cube + u_s[f] * w_s[f]
+    for f in matrix:
+        beam_part = beam_part + seen[f][0] * seen[f][1]
     lane = lax.broadcasted_iota(jnp.int32, (1, 128), 1)
     message = jnp.zeros((1, 128), F32)
-    for i, part in enumerate((norm, curve, square, cube)):
+    for i, part in enumerate(sums):
         total = total_of(part)
         if i == 3:
             total = total + total_of(beam_part) + jnp.sum(column_part, axis=0, keepdims=True)

time: 15.7 us -> 15.7 us (level)
  no operation moved by 1% of the time
where the time goes in v12:
time: 15.7 us; the launch traced here: 15.6 us
  Pallas kernels  14.9 us (95%)
  between operations  0.64 us (4%)
    pallas_call x1, Pallas kernels, shards(): pl.pallas_call(functools.partial(scoped_kernel, nma, nf, sides), out_shap...  14.2 us
    pallas_call x1, Pallas kernels, shards(): pl.pallas_call(write_out, out_shape=[jax.ShapeDtypeStruct(right_side.shap...  0.72 us

profile of v12, /device:TPU:0, one launch (start us, length us, event | category | flops | bytes accessed | tf_op | source)
XLA Modules:
  0.0 15.6 jit_solution(5567139803149974260)
XLA Ops:
  0.6 14.2 %solve.1 = (f32[8,4,2,512]{3,2,1,0:T(2,128)S(1)}, f32[8,4,2,512]{3,2,1,0:T(2,128)S(1)}) custom-call(f32[8,4,2,512]{3,2,1,0:T(2,128)} %refs_0_.1, f32[8,4,2,512]{3,2,1,0:T(2,128)} %refs_1_.1, f32[8,4,2,16,512]{4,3,2,1,0:T(8,128)} %refs_2_.1, f32[8,4,16]{2,1,0:T(4,128)} %refs_3_.1, f32[1,512]{1,0:T(1,128)} %bitcast.2, f32[1,512]{1,0:T(1,128)} %bitcast.3), custom_call_target="tpu_custom_call" | custom-call | tf_op jit(solution)/shard_map/solve/pallas_call | solution.py:716
  14.8 0.7 %write_out.1 = (f32[8,4,2,512]{3,2,1,0:T(2,128)}, f32[8,4,2,512]{3,2,1,0:T(2,128)}) custom-call(f32[8,4,2,512]{3,2,1,0:T(2,128)S(1)} %get-tuple-element.4.sol_in, f32[8,4,2,512]{3,2,1,0:T(2,128)S(1)} %get-tuple-element.5.res_in), custom_call_target="tpu_custom_call" | custom-call | tf_op jit(solution)/shard_map/write_out/pallas_call | solution.py:749

commit v13 on v12

--- a/solution.py
+++ b/solution.py
@@ -44,6 +44,13 @@
     return jnp.where(
         row % 2 == 0, twos[0] + pltpu.roll(twos[0], 7, 0), twos[1] + pltpu.roll(twos[1], 1, 0)
     )
+
+
+def tree(parts):
+    while len(parts) > 1:
+        half = len(parts) // 2
+        parts = [parts[k] + parts[half + k] for k in range(half)] + parts[2 * half:]
+    return parts[0]
 
 
 def total_of(x):
@@ -99,6 +106,8 @@
         copy.start()
 
     def flip(bit):
+        if bit == 0 and nf == 2:
+            return 1 - 2 * my_f
         d = 1 << (bit if bit < freq_bits else bit - freq_bits)
         place = my_f if bit < freq_bits else my_ma
         return d * (1 - 2 * (place // d % 2))
@@ -656,12 +665,17 @@
     else:
         landed(late_s, sum_send.at[1], late_rows - 1)
         landed(late_s, sum_recv.at[1], late_rows - 1)
-    total = jnp.sum(early_s[...], axis=0)
+    def rows_total(ref):
+        if ref.shape[0] > 64:
+            return jnp.sum(ref[...], axis=0)
+        return tree([ref[k] for k in range(ref.shape[0])])
+
+    total = rows_total(early_s)
     m0, m1, m2, m3, known = (
         jnp.sum(jnp.where(lane == i, total, 0.0), axis=1, keepdims=True)
         for i in (0, 1, 2, 3, 4 + my_f)
     )
-    crossed = jnp.sum(jnp.sum(late_s[...], axis=0), axis=1, keepdims=True)
+    crossed = jnp.sum(rows_total(late_s), axis=1, keepdims=True)
     m3 = m3 - 2.0 * (crossed - known) if paired else m3 - crossed
     inverse = 1.0 / m1
     step = m0 * inverse
@@ -671,9 +685,10 @@
     step_next = step * drop / (curve_next - growth * drop)
     c = step + step_next * (1.0 + growth)
     e = step * step_next
-    r, u = r_out_s[...], u_out_s[...]
-    sol_s[...] = x0_s[...] + c * r - e * u
-    res_s[...] = r - c * u + e * w_out_s[...]
+    for m in range(modes):
+        r, u = r_out_s[m], u_out_s[m]
+        sol_s[m] = x0_s[m] + c * r - e * u
+        res_s[m] = r - c * u + e * w_out_s[m]
 
 
 def scoped_kernel(nma, nf, sides, *refs):

time: 15.7 us -> 15.7 us (level)
  no operation moved by 1% of the time
where the time goes in v13:
time: 15.7 us; the launch traced here: 15.5 us
  Pallas kernels  14.9 us (95%)
  between operations  0.64 us (4%)
    pallas_call x1, Pallas kernels, shards(): pl.pallas_call(functools.partial(scoped_kernel, nma, nf, sides), out_shap...  14.2 us
    pallas_call x1, Pallas kernels, shards(): pl.pallas_call(write_out, out_shape=[jax.ShapeDtypeStruct(right_side.shap...  0.72 us

profile of v13, /device:TPU:0, one launch (start us, length us, event | category | flops | bytes accessed | tf_op | source)
XLA Modules:
  0.0 15.5 jit_solution(14186097577351429230)
XLA Ops:
  0.6 14.2 %solve.1 = (f32[8,4,2,512]{3,2,1,0:T(2,128)S(1)}, f32[8,4,2,512]{3,2,1,0:T(2,128)S(1)}) custom-call(f32[8,4,2,512]{3,2,1,0:T(2,128)} %refs_0_.1, f32[8,4,2,512]{3,2,1,0:T(2,128)} %refs_1_.1, f32[8,4,2,16,512]{4,3,2,1,0:T(8,128)} %refs_2_.1, f32[8,4,16]{2,1,0:T(4,128)} %refs_3_.1, f32[1,512]{1,0:T(1,128)} %bitcast.2, f32[1,512]{1,0:T(1,128)} %bitcast.3), custom_call_target="tpu_custom_call" | custom-call | tf_op jit(solution)/shard_map/solve/pallas_call | solution.py:731
  14.8 0.7 %write_out.1 = (f32[8,4,2,512]{3,2,1,0:T(2,128)}, f32[8,4,2,512]{3,2,1,0:T(2,128)}) custom-call(f32[8,4,2,512]{3,2,1,0:T(2,128)S(1)} %get-tuple-element.4.sol_in, f32[8,4,2,512]{3,2,1,0:T(2,128)S(1)} %get-tuple-element.5.res_in), custom_call_target="tpu_custom_call" | custom-call | tf_op jit(solution)/shard_map/write_out/pallas_call | solution.py:764

commit v14 on v13

--- a/solution.py
+++ b/solution.py
@@ -265,10 +265,7 @@
     if paired:
         even_only([first_copy(g) for g in range(groups)])
 
-        @pl.when(helper)
-        def _():
-            for g in range(groups):
-                near_copy(0, g).start()
+        pl.when(helper)(lambda: near_copy(0, 0).start())
     else:
         for g in range(groups):
             send(0, g)
@@ -405,6 +402,12 @@
     first, rest = [], inner
     if paired:
         even_only([near_copy(1, g) for g in range(groups)] + [lend(k) for k in range(3)])
+
+        @pl.when(helper)
+        def _():
+            for g in range(1, groups):
+                near_copy(0, g).start()
+
         first, rest = inner[:1], inner[1:]
     else:
         for g in range(groups):
@@ -701,15 +704,18 @@
     )
 
 
-def write_out(sol_in, res_in, sol_out, res_out, sem):
-    copies = [
-        pltpu.make_async_copy(sol_in, sol_out, sem.at[0]),
-        pltpu.make_async_copy(res_in, res_out, sem.at[1]),
-    ]
-    for copy in copies:
-        copy.start()
-    for copy in copies:
-        copy.wait()
+def write_out(sol_in, res_in, sol_out, res_out):
+    def body(sem):
+        copies = [
+            pltpu.make_async_copy(sol_in, sol_out, sem.at[0]),
+            pltpu.make_async_copy(res_in, res_out, sem.at[1]),
+        ]
+        for copy in copies:
+            copy.start()
+        for copy in copies:
+            copy.wait()
+
+    pl.run_scoped(body, pltpu.SemaphoreType.DMA((2,)))
 
 
 def shards(right_side, start_field, beam, noise, inv_power, smooth):
@@ -766,7 +772,6 @@
         out_shape=[jax.ShapeDtypeStruct(right_side.shape, F32)] * 2,
         in_specs=[vmem_spec] * 2,
         out_specs=[any_spec] * 2,
-        scratch_shapes=[pltpu.SemaphoreType.DMA((2,))],
         compiler_params=pltpu.CompilerParams(vmem_limit_bytes=1024 * 1024),
         name="write_out",
     )(*outs)

time: 15.7 us -> 15.6 us (level)
  no operation moved by 1% of the time
where the time goes in v14:
time: 15.6 us; the launch traced here: 15.5 us
  Pallas kernels  14.9 us (96%)
  between operations  0.64 us (4%)
    pallas_call x1, Pallas kernels, shards(): pl.pallas_call(functools.partial(scoped_kernel, nma, nf, sides), out_shap...  14.2 us
    pallas_call x1, Pallas kernels, shards(): pl.pallas_call(write_out, out_shape=[jax.ShapeDtypeStruct(right_side.shap...  0.7 us

profile of v14, /device:TPU:0, one launch (start us, length us, event | category | flops | bytes accessed | tf_op | source)
XLA Modules:
  0.0 15.5 jit_solution(8368445200904500447)
XLA Ops:
  0.6 14.2 %solve.1 = (f32[8,4,2,512]{3,2,1,0:T(2,128)S(1)}, f32[8,4,2,512]{3,2,1,0:T(2,128)S(1)}) custom-call(f32[8,4,2,512]{3,2,1,0:T(2,128)} %refs_0_.1, f32[8,4,2,512]{3,2,1,0:T(2,128)} %refs_1_.1, f32[8,4,2,16,512]{4,3,2,1,0:T(8,128)} %refs_2_.1, f32[8,4,16]{2,1,0:T(4,128)} %refs_3_.1, f32[1,512]{1,0:T(1,128)} %bitcast.2, f32[1,512]{1,0:T(1,128)} %bitcast.3), custom_call_target="tpu_custom_call" | custom-call | tf_op jit(solution)/shard_map/solve/pallas_call | solution.py:737
  14.8 0.7 %write_out.1 = (f32[8,4,2,512]{3,2,1,0:T(2,128)}, f32[8,4,2,512]{3,2,1,0:T(2,128)}) custom-call(f32[8,4,2,512]{3,2,1,0:T(2,128)S(1)} %get-tuple-element.4.sol_in, f32[8,4,2,512]{3,2,1,0:T(2,128)S(1)} %get-tuple-element.5.res_in), custom_call_target="tpu_custom_call" | custom-call | tf_op jit(solution)/shard_map/write_out/pallas_call | solution.py:770

commit v15 on v14

--- a/solution.py
+++ b/solution.py
@@ -121,24 +121,25 @@
     freq_bits = nf.bit_length() - 1
     bits = freq_bits + nma.bit_length() - 1
     close = min(bits, 3)
-    greeted = [
-        partner([bit for bit in range(close) if mask >> bit & 1]) for mask in range(1, 1 << close)
-    ]
+    barrier = pltpu.get_barrier_semaphore()
+
+    def greet(device):
+        pl.semaphore_signal(barrier, inc=1, device_id=device, device_id_type=MESH)
+
+    greeted = []
+    for mask in range(1, 1 << close):
+        greeted.append(partner([bit for bit in range(close) if mask >> bit & 1]))
+        greet(greeted[-1])
+        if mask == 1:
+            for copy in [beam_copies[f] for f in edges] + [x0_copy, rhs_copy] + small:
+                copy.start()
     word = [partner([bit]) for bit in range(close, bits)]
+    for device in word:
+        greet(device)
     greeted += word
     words = len(word)
-    barrier = pltpu.get_barrier_semaphore()
     near = jnp.where(my_f == 0, 1, my_f - 1)
     has_far = (my_f > 0) & (my_f < nf - 1)
-
-    def greet(device):
-        pl.semaphore_signal(barrier, inc=1, device_id=device, device_id_type=MESH)
-
-    for i, device in enumerate(greeted):
-        greet(device)
-        if i == 0:
-            for copy in [beam_copies[f] for f in edges] + [x0_copy, rhs_copy] + small:
-                copy.start()
     expected = len(greeted)
     if nf > 2:
         pl.when(my_f > 0)(lambda: greet((my_ma, my_f - 1)))

time: 15.6 us -> 15.6 us (level)
  no operation moved by 1% of the time
where the time goes in v15:
time: 15.6 us; the launch traced here: 15.5 us
  Pallas kernels  14.8 us (95%)
  between operations  0.64 us (4%)
    pallas_call x1, Pallas kernels, shards(): pl.pallas_call(functools.partial(scoped_kernel, nma, nf, sides), out_shap...  14.1 us
    pallas_call x1, Pallas kernels, shards(): pl.pallas_call(write_out, out_shape=[jax.ShapeDtypeStruct(right_side.shap...  0.7 us

profile of v15, /device:TPU:0, one launch (start us, length us, event | category | flops | bytes accessed | tf_op | source)
XLA Modules:
  0.0 15.5 jit_solution(14780310233696677621)
XLA Ops:
  0.6 14.1 %solve.1 = (f32[8,4,2,512]{3,2,1,0:T(2,128)S(1)}, f32[8,4,2,512]{3,2,1,0:T(2,128)S(1)}) custom-call(f32[8,4,2,512]{3,2,1,0:T(2,128)} %refs_0_.1, f32[8,4,2,512]{3,2,1,0:T(2,128)} %refs_1_.1, f32[8,4,2,16,512]{4,3,2,1,0:T(8,128)} %refs_2_.1, f32[8,4,16]{2,1,0:T(4,128)} %refs_3_.1, f32[1,512]{1,0:T(1,128)} %bitcast.2, f32[1,512]{1,0:T(1,128)} %bitcast.3), custom_call_target="tpu_custom_call" | custom-call | tf_op jit(solution)/shard_map/solve/pallas_call | solution.py:738
  14.8 0.7 %write_out.1 = (f32[8,4,2,512]{3,2,1,0:T(2,128)}, f32[8,4,2,512]{3,2,1,0:T(2,128)}) custom-call(f32[8,4,2,512]{3,2,1,0:T(2,128)S(1)} %get-tuple-element.4.sol_in, f32[8,4,2,512]{3,2,1,0:T(2,128)S(1)} %get-tuple-element.5.res_in), custom_call_target="tpu_custom_call" | custom-call | tf_op jit(solution)/shard_map/write_out/pallas_call | solution.py:771

commit v16 on v15

--- a/solution.py
+++ b/solution.py
@@ -74,7 +74,7 @@
     me = my_ma * nf + my_f
     last = freqs - 1
     two_sided = nf > 2
-    paired = nf == 2 and nma % 2 == 0 and freqs > 1
+    paired = nf == 2 and nma % 2 == 0 and freqs > 3
     helper = my_ma % 2 == 1
     groups = modes // 4
     edges = [0, last][:min(nf - 1, 2)]
@@ -757,7 +757,7 @@
             edge_field, edge_field, pltpu.VMEM((modes, 2, ell), F32), edge_field, edge_field,
             pltpu.VMEM((2, 1, 128), F32),
             pltpu.VMEM((nma * nf, 1, 128), F32),
-            pltpu.VMEM((nma // 2 if nf == 2 and nma % 2 == 0 and freqs > 1 else nma * nf, 1, 128), F32),
+            pltpu.VMEM((nma // 2 if nf == 2 and nma % 2 == 0 and freqs > 3 else nma * nf, 1, 128), F32),
             pltpu.SemaphoreType.DMA((3, modes // 4, sides)),
             pltpu.SemaphoreType.DMA((2 * (modes // 4) + 5,)),
             pltpu.SemaphoreType.DMA((2,)),

time: 15.6 us -> 15.6 us (level)
  no operation moved by 1% of the time
where the time goes in v16:
time: 15.6 us; the launch traced here: 15.5 us
  Pallas kernels  14.8 us (95%)
  between operations  0.64 us (4%)
    pallas_call x1, Pallas kernels, shards(): pl.pallas_call(functools.partial(scoped_kernel, nma, nf, sides), out_shap...  14.1 us
    pallas_call x1, Pallas kernels, shards(): pl.pallas_call(write_out, out_shape=[jax.ShapeDtypeStruct(right_side.shap...  0.7 us

profile of v16, /device:TPU:0, one launch (start us, length us, event | category | flops | bytes accessed | tf_op | source)
XLA Modules:
  0.0 15.5 jit_solution(14780310233696677621)
XLA Ops:
  0.6 14.1 %solve.1 = (f32[8,4,2,512]{3,2,1,0:T(2,128)S(1)}, f32[8,4,2,512]{3,2,1,0:T(2,128)S(1)}) custom-call(f32[8,4,2,512]{3,2,1,0:T(2,128)} %refs_0_.1, f32[8,4,2,512]{3,2,1,0:T(2,128)} %refs_1_.1, f32[8,4,2,16,512]{4,3,2,1,0:T(8,128)} %refs_2_.1, f32[8,4,16]{2,1,0:T(4,128)} %refs_3_.1, f32[1,512]{1,0:T(1,128)} %bitcast.2, f32[1,512]{1,0:T(1,128)} %bitcast.3), custom_call_target="tpu_custom_call" | custom-call | tf_op jit(solution)/shard_map/solve/pallas_call | solution.py:738
  14.8 0.7 %write_out.1 = (f32[8,4,2,512]{3,2,1,0:T(2,128)}, f32[8,4,2,512]{3,2,1,0:T(2,128)}) custom-call(f32[8,4,2,512]{3,2,1,0:T(2,128)S(1)} %get-tuple-element.4.sol_in, f32[8,4,2,512]{3,2,1,0:T(2,128)S(1)} %get-tuple-element.5.res_in), custom_call_target="tpu_custom_call" | custom-call | tf_op jit(solution)/shard_map/write_out/pallas_call | solution.py:771

commit v17 on v16

--- a/solution.py
+++ b/solution.py
@@ -658,17 +658,6 @@
 
     landed(early_s, sum_send.at[0], n - 1)
     landed(early_s, sum_recv.at[0], n - 1)
-    if paired:
-        @pl.when(helper)
-        def _():
-            rows = early_s.at[pl.ds(0, nma - 1)]
-            pltpu.make_async_copy(rows, rows, sum_send.at[1]).wait()
-            landed(late_s, sum_recv.at[1], late_rows - 1)
-
-        pl.when(jnp.logical_not(helper))(lambda: landed(late_s, sum_recv.at[1], late_rows))
-    else:
-        landed(late_s, sum_send.at[1], late_rows - 1)
-        landed(late_s, sum_recv.at[1], late_rows - 1)
     def rows_total(ref):
         if ref.shape[0] > 64:
             return jnp.sum(ref[...], axis=0)
@@ -679,12 +668,23 @@
         jnp.sum(jnp.where(lane == i, total, 0.0), axis=1, keepdims=True)
         for i in (0, 1, 2, 3, 4 + my_f)
     )
-    crossed = jnp.sum(rows_total(late_s), axis=1, keepdims=True)
-    m3 = m3 - 2.0 * (crossed - known) if paired else m3 - crossed
     inverse = 1.0 / m1
     step = m0 * inverse
     drop = step * m2 - m1
     growth = drop * inverse
+    if paired:
+        @pl.when(helper)
+        def _():
+            rows = early_s.at[pl.ds(0, nma - 1)]
+            pltpu.make_async_copy(rows, rows, sum_send.at[1]).wait()
+            landed(late_s, sum_recv.at[1], late_rows - 1)
+
+        pl.when(jnp.logical_not(helper))(lambda: landed(late_s, sum_recv.at[1], late_rows))
+    else:
+        landed(late_s, sum_send.at[1], late_rows - 1)
+        landed(late_s, sum_recv.at[1], late_rows - 1)
+    crossed = jnp.sum(rows_total(late_s), axis=1, keepdims=True)
+    m3 = m3 - 2.0 * (crossed - known) if paired else m3 - crossed
     curve_next = m1 - 2.0 * step * m2 + step * step * m3
     step_next = step * drop / (curve_next - growth * drop)
     c = step + step_next * (1.0 + growth)

time: 15.6 us -> 15.6 us (level)
  no operation moved by 1% of the time
where the time goes in v17:
time: 15.6 us; the launch traced here: 15.5 us
  Pallas kernels  14.8 us (95%)
  between operations  0.64 us (4%)
    pallas_call x1, Pallas kernels, shards(): pl.pallas_call(functools.partial(scoped_kernel, nma, nf, sides), out_shap...  14.1 us
    pallas_call x1, Pallas kernels, shards(): pl.pallas_call(write_out, out_shape=[jax.ShapeDtypeStruct(right_side.shap...  0.7 us

profile of v17, /device:TPU:0, one launch (start us, length us, event | category | flops | bytes accessed | tf_op | source)
XLA Modules:
  0.0 15.5 jit_solution(8013612104048286726)
XLA Ops:
  0.6 14.1 %solve.1 = (f32[8,4,2,512]{3,2,1,0:T(2,128)S(1)}, f32[8,4,2,512]{3,2,1,0:T(2,128)S(1)}) custom-call(f32[8,4,2,512]{3,2,1,0:T(2,128)} %refs_0_.1, f32[8,4,2,512]{3,2,1,0:T(2,128)} %refs_1_.1, f32[8,4,2,16,512]{4,3,2,1,0:T(8,128)} %refs_2_.1, f32[8,4,16]{2,1,0:T(4,128)} %refs_3_.1, f32[1,512]{1,0:T(1,128)} %bitcast.2, f32[1,512]{1,0:T(1,128)} %bitcast.3), custom_call_target="tpu_custom_call" | custom-call | tf_op jit(solution)/shard_map/solve/pallas_call | solution.py:738
  14.8 0.7 %write_out.1 = (f32[8,4,2,512]{3,2,1,0:T(2,128)}, f32[8,4,2,512]{3,2,1,0:T(2,128)}) custom-call(f32[8,4,2,512]{3,2,1,0:T(2,128)S(1)} %get-tuple-element.4.sol_in, f32[8,4,2,512]{3,2,1,0:T(2,128)S(1)} %get-tuple-element.5.res_in), custom_call_target="tpu_custom_call" | custom-call | tf_op jit(solution)/shard_map/write_out/pallas_call | solution.py:771
